TPU v7x, 256 devices: a whole 4x4x8 slice. The times are simulated.
256 devices in a mesh: seq: 16 (over x, y_lo, core), exp: 16 (over y_hi, z).
Axes of the slice: x: 4, y: 4 (y_hi: 2, y_lo: 2; y = y_hi * 2 + y_lo), z: 8, core: 2. Of those that a mesh axis runs over, the one named last changes fastest.
Arguments:
- queries: bfloat16 [8, 4096, 2048], P(None, 'seq', 'exp'), may hold values from -5 to 5
- keys: bfloat16 [8, 4096, 2048], P(None, 'seq', 'exp'), may hold values from -5 to 5
- values: bfloat16 [8, 4096, 2048], P(None, 'seq', 'exp'), may hold values from -170 to 170
- seg_ids: int32 [8, 4096], replicated, may hold values from 0 to 3, as said below
- norm_gain: float32 [2048], replicated, may hold values from 0.25 to 1.75
- router_w: bfloat16 [512, 64], replicated, may hold values from -0.25 to 0.25
- expert_ids: int32 [4096, 8, 4, 2], P(('seq', 'exp')), may hold values from 0 to 63, all different within a row; in each aligned block of 512 rows (0 to 511, 512 to 1023, ..., all dimensions but the last counted through in order) at most 32 rows name the same one
- w_in: bfloat16 [64, 512, 1024], P('exp'), may hold values from -0.25 to 0.25
- w_out: bfloat16 [64, 1024, 512], P('exp'), may hold values from -0.1875 to 0.1875
Outputs:
- normed: bfloat16 [8, 4096, 2048], P(None, ('seq', 'exp'))
- expert_mix: bfloat16 [8, 4096, 2048], P(None, ('seq', 'exp'))
Inputs may be any that keep to these rules, and one draw needn't show every extreme that they name: `seg_ids`: in each sequence the numbers start at 0, never fall, and rise by one at each of 3 document starts; every start lies at an even position after the middle of the sequence. `expert_ids`: the 2 experts of a sub-token differ. Among the rows of one device (its 16 positions, all sequences, all sub-tokens) no expert is named more than 32 times; in every draw some device names some expert exactly 32 times.
All inputs are finite; a program needn't handle non-finite values.
Results may differ from a plain program's by a relative error of at most 0.015.
Values may be sent and summed in bfloat16 or wider, within the bound.
A program may use at most 128 MiB of HBM per device.

v0:
```python
import jax
import jax.numpy as jnp
from jax import lax
from jax.sharding import PartitionSpec as P

HD = 128
SUB = 512
TOPK = 2
CAP = 32


NEG = -1e30


def update(running, query_heads, shaped, query_pos, query_seg, key_pos, key_seg, score_scale):
    maxima, totals, running_total = running
    attention_scores = (
        jnp.einsum("bqhd,bkhd->bhqk", query_heads, shaped[0], preferred_element_type=jnp.float32)
        * score_scale
    )
    visible = (key_pos[None, :] <= query_pos[:, None])[None, None] & (
        key_seg[:, None, None, :] == query_seg[:, None, :, None]
    )
    highest = jnp.max(jnp.where(visible, attention_scores, NEG), axis=-1)
    new_max = jnp.maximum(maxima, highest)
    weights = jnp.where(visible, jnp.exp(attention_scores - new_max[..., None]), 0.0)
    rescale_factor = jnp.exp(maxima - new_max)
    totals = totals * rescale_factor + jnp.sum(weights, axis=-1)
    rounded_result = weights.astype(jnp.bfloat16)
    running_total = running_total * rescale_factor[..., None] + jnp.einsum(
        "bhqk,bkhd->bhqd", rounded_result, shaped[1], preferred_element_type=jnp.float32
    )
    return (new_max, totals, running_total)


def attend_block(
    running, query_heads, block, query_pos, query_seg, seg_ids, key_first, score_scale
):
    row_count = block.shape[2]
    key_pos = key_first + jnp.arange(row_count, dtype=jnp.int32)
    key_seg = lax.dynamic_slice_in_dim(seg_ids, key_first, row_count, 1)
    needed = (key_first <= query_pos[-1]) & jnp.any(key_seg[:, -1] >= query_seg[:, 0])
    shaped = block.reshape(2, block.shape[1], row_count, query_heads.shape[2], query_heads.shape[3])
    return lax.cond(
        needed,
        lambda state: update(
            state, query_heads, shaped, query_pos, query_seg, key_pos, key_seg, score_scale
        ),
        lambda state: state,
        running,
    )


def body(queries, keys, values, seg_ids, norm_gain, router_w, expert_ids, w_in, w_out):
    my_index = lax.axis_index("seq")
    seq_count, local_len, local_width = queries.shape
    head_count = local_width // HD
    score_scale = HD ** (-0.5)
    first_pos = my_index * local_len
    query_pos = first_pos + jnp.arange(local_len, dtype=jnp.int32)
    query_seg = lax.dynamic_slice_in_dim(seg_ids, first_pos, local_len, 1)
    query_heads = queries.reshape(seq_count, local_len, head_count, HD)
    initial = (
        jnp.full((seq_count, head_count, local_len), NEG, jnp.float32),
        jnp.zeros((seq_count, head_count, local_len), jnp.float32),
        jnp.zeros((seq_count, head_count, local_len, HD), jnp.float32),
    )
    stacked = jnp.stack([keys, values])

    def attend(running, block, key_first):
        return attend_block(
            running, query_heads, block, query_pos, query_seg, seg_ids, key_first, score_scale
        )

    shard_part = lax.all_gather(stacked, "seq", axis=2, tiled=True)
    row_count = shard_part.shape[2]
    width = min(row_count, local_len)
    repeats = row_count // width

    def inner(number, state):
        section = lax.dynamic_slice_in_dim(shard_part, number * width, width, 2)
        return attend(state, section, number * width)

    running = lax.fori_loop(0, repeats, inner, initial)
    maxima, totals, running_total = running
    attended = (
        (running_total / totals[..., None])
        .transpose(0, 2, 1, 3)
        .reshape(seq_count, local_len, local_width)
        .astype(jnp.bfloat16)
    )
    tokens = lax.all_to_all(attended, "exp", split_axis=1, concat_axis=2, tiled=True)
    values32 = tokens.astype(jnp.float32)
    spread = jnp.sqrt(jnp.mean(values32 * values32, axis=-1, keepdims=True) + 1e-06)
    normed = (values32 / spread * norm_gain).astype(jnp.bfloat16)
    token_count = normed.shape[1]
    feature_count = normed.shape[2]
    sub_count = feature_count // SUB
    sub_rows = (
        normed.reshape(seq_count, token_count, sub_count, SUB)
        .transpose(1, 0, 2, 3)
        .reshape(-1, SUB)
    )
    picks = expert_ids.reshape(-1, TOPK)
    logits = jnp.dot(sub_rows, router_w, preferred_element_type=jnp.float32)
    chosen = jnp.take_along_axis(logits, picks, axis=1)
    sigmas = jax.nn.sigmoid(chosen)
    gates = sigmas / jnp.sum(sigmas, axis=1, keepdims=True)
    expert_total = router_w.shape[1]
    targets = picks.reshape(-1)
    one_hot = (targets[:, None] == jnp.arange(expert_total, dtype=jnp.int32)[None, :]).astype(
        jnp.int32
    )
    earlier = jnp.cumsum(one_hot, axis=0) - one_hot
    slot_rank = jnp.sum(earlier * one_hot, axis=1)
    destination = targets * CAP + slot_rank
    sources = jnp.arange(targets.shape[0], dtype=jnp.int32) // TOPK
    outgoing = (
        jnp.zeros((expert_total * CAP, SUB), jnp.bfloat16)
        .at[destination]
        .set(sub_rows[sources])
        .reshape(expert_total, CAP, SUB)
    )
    arrived = lax.all_to_all(outgoing, "exp", split_axis=0, concat_axis=1, tiled=True)
    hidden = jax.nn.gelu(
        jnp.einsum("ecs,esf->ecf", arrived, w_in, preferred_element_type=jnp.float32),
        approximate=True,
    ).astype(jnp.bfloat16)
    results = jnp.einsum("ecf,efs->ecs", hidden, w_out, preferred_element_type=jnp.float32).astype(
        jnp.bfloat16
    )
    returned = lax.all_to_all(results, "exp", split_axis=1, concat_axis=0, tiled=True).reshape(
        expert_total * CAP, SUB
    )
    picked = returned[destination].reshape(-1, TOPK, SUB).astype(jnp.float32)
    mixed = jnp.sum(gates[:, :, None] * picked, axis=1).astype(jnp.bfloat16)
    expert_mix = mixed.reshape(token_count, seq_count, feature_count).transpose(1, 0, 2)
    return (normed, expert_mix)


def solution(mesh):
    return jax.shard_map(
        body,
        mesh=mesh,
        in_specs=(
            P(None, "seq", "exp"),
            P(None, "seq", "exp"),
            P(None, "seq", "exp"),
            P(),
            P(),
            P(),
            P(("seq", "exp"), None, None, None),
            P("exp", None, None),
            P("exp", None, None),
        ),
        out_specs=(P(None, ("seq", "exp"), None), P(None, ("seq", "exp"), None)),
        check_vma=False,
    )
```

profile of v0, /device:TPU:13, one launch (start us, length us, event | category | flops | bytes accessed | tf_op | source)
XLA Modules:
  0.0 475.9 jit_solution(5540001684064581826)
XLA Ops:
  12.8 94.1 %all-gather.2.cloned.1.call-done = bf16[2,8,4096,128]{3,2,1,0:T(8,128)(2,1)} async-done(((bf16[2,8,256,128]{3,2,1,0:T(8,128)(2,1)}), bf16[2,8,4096,128]{3,2,1,0:T(8,128)(2,1)}) %all-gather.2.cloned.1.call-update) | async-done | bytes 16777232 | tf_op jit(solution)/shard_map/all_gather | solution.py:75
  107.6 180.6 %while.17 = (s32[]{:T(128)}, f32[8,1,256]{2,0,1:T(8,128)S(1)}, f32[8,1,256]{2,0,1:T(8,128)}, f32[8,1,256,128]{3,2,0,1:T(8,128)S(1)}, s32[256]{0:T(256)}, /*index...) while((s32[]{:T(128)}, f32[8,1,256]{2,0,1:T(8,128)S(1)}, ...), condition=%wide.region_6.7_spmd, body=%wide.region_0.6_spmd.sunk | while | flops 277944608 | bytes 10492413 | solution.py:84
  112.2 8.8 %conditional.2 = ((f32[8,1,256]{2,0,1:T(8,128)S(1)}, f32[8,1,256]{2,0,1:T(8,128)}, f32[8,1,256,128]{3,2,0,1:T(8,128)S(1)})) conditional(s32[]{:T(128)} %convert_element_type.119, (f32[8,1,256]{2,0,1:T(8,128)S(1)}, f32[8,1,256]{2,0,1:T(8,128)}, f32[8,1,256,128]{3,2,0,1:T(8,128)S(1)}) %tuple.51, (s32[]{:T(128)}, s32[256]{0:T(256)S(1)}, s32[256]{0:T(256)}, ...), branch_computations={%region_2.0_spmd, %region_3.5_spmd} | conditional | flops 277944576 | bytes 10474604 | solution.py:44
  125.7 8.8 %conditional.2 = ((f32[8,1,256]{2,0,1:T(8,128)S(1)}, f32[8,1,256]{2,0,1:T(8,128)}, f32[8,1,256,128]{3,2,0,1:T(8,128)S(1)})) conditional(s32[]{:T(128)} %convert_element_type.119, (f32[8,1,256]{2,0,1:T(8,128)S(1)}, f32[8,1,256]{2,0,1:T(8,128)}, f32[8,1,256,128]{3,2,0,1:T(8,128)S(1)}) %tuple.51, (s32[]{:T(128)}, s32[256]{0:T(256)S(1)}, s32[256]{0:T(256)}, ...), branch_computations={%region_2.0_spmd, %region_3.5_spmd} | conditional | flops 277944576 | bytes 10474604 | solution.py:44
  139.2 8.8 %conditional.2 = ((f32[8,1,256]{2,0,1:T(8,128)S(1)}, f32[8,1,256]{2,0,1:T(8,128)}, f32[8,1,256,128]{3,2,0,1:T(8,128)S(1)})) conditional(s32[]{:T(128)} %convert_element_type.119, (f32[8,1,256]{2,0,1:T(8,128)S(1)}, f32[8,1,256]{2,0,1:T(8,128)}, f32[8,1,256,128]{3,2,0,1:T(8,128)S(1)}) %tuple.51, (s32[]{:T(128)}, s32[256]{0:T(256)S(1)}, s32[256]{0:T(256)}, ...), branch_computations={%region_2.0_spmd, %region_3.5_spmd} | conditional | flops 277944576 | bytes 10474604 | solution.py:44
  152.7 8.8 %conditional.2 = ((f32[8,1,256]{2,0,1:T(8,128)S(1)}, f32[8,1,256]{2,0,1:T(8,128)}, f32[8,1,256,128]{3,2,0,1:T(8,128)S(1)})) conditional(s32[]{:T(128)} %convert_element_type.119, (f32[8,1,256]{2,0,1:T(8,128)S(1)}, f32[8,1,256]{2,0,1:T(8,128)}, f32[8,1,256,128]{3,2,0,1:T(8,128)S(1)}) %tuple.51, (s32[]{:T(128)}, s32[256]{0:T(256)S(1)}, s32[256]{0:T(256)}, ...), branch_computations={%region_2.0_spmd, %region_3.5_spmd} | conditional | flops 277944576 | bytes 10474604 | solution.py:44
  166.1 8.8 %conditional.2 = ((f32[8,1,256]{2,0,1:T(8,128)S(1)}, f32[8,1,256]{2,0,1:T(8,128)}, f32[8,1,256,128]{3,2,0,1:T(8,128)S(1)})) conditional(s32[]{:T(128)} %convert_element_type.119, (f32[8,1,256]{2,0,1:T(8,128)S(1)}, f32[8,1,256]{2,0,1:T(8,128)}, f32[8,1,256,128]{3,2,0,1:T(8,128)S(1)}) %tuple.51, (s32[]{:T(128)}, s32[256]{0:T(256)S(1)}, s32[256]{0:T(256)}, ...), branch_computations={%region_2.0_spmd, %region_3.5_spmd} | conditional | flops 277944576 | bytes 10474604 | solution.py:44
  179.6 8.8 %conditional.2 = ((f32[8,1,256]{2,0,1:T(8,128)S(1)}, f32[8,1,256]{2,0,1:T(8,128)}, f32[8,1,256,128]{3,2,0,1:T(8,128)S(1)})) conditional(s32[]{:T(128)} %convert_element_type.119, (f32[8,1,256]{2,0,1:T(8,128)S(1)}, f32[8,1,256]{2,0,1:T(8,128)}, f32[8,1,256,128]{3,2,0,1:T(8,128)S(1)}) %tuple.51, (s32[]{:T(128)}, s32[256]{0:T(256)S(1)}, s32[256]{0:T(256)}, ...), branch_computations={%region_2.0_spmd, %region_3.5_spmd} | conditional | flops 277944576 | bytes 10474604 | solution.py:44
  193.1 8.8 %conditional.2 = ((f32[8,1,256]{2,0,1:T(8,128)S(1)}, f32[8,1,256]{2,0,1:T(8,128)}, f32[8,1,256,128]{3,2,0,1:T(8,128)S(1)})) conditional(s32[]{:T(128)} %convert_element_type.119, (f32[8,1,256]{2,0,1:T(8,128)S(1)}, f32[8,1,256]{2,0,1:T(8,128)}, f32[8,1,256,128]{3,2,0,1:T(8,128)S(1)}) %tuple.51, (s32[]{:T(128)}, s32[256]{0:T(256)S(1)}, s32[256]{0:T(256)}, ...), branch_computations={%region_2.0_spmd, %region_3.5_spmd} | conditional | flops 277944576 | bytes 10474604 | solution.py:44
  206.6 8.8 %conditional.2 = ((f32[8,1,256]{2,0,1:T(8,128)S(1)}, f32[8,1,256]{2,0,1:T(8,128)}, f32[8,1,256,128]{3,2,0,1:T(8,128)S(1)})) conditional(s32[]{:T(128)} %convert_element_type.119, (f32[8,1,256]{2,0,1:T(8,128)S(1)}, f32[8,1,256]{2,0,1:T(8,128)}, f32[8,1,256,128]{3,2,0,1:T(8,128)S(1)}) %tuple.51, (s32[]{:T(128)}, s32[256]{0:T(256)S(1)}, s32[256]{0:T(256)}, ...), branch_computations={%region_2.0_spmd, %region_3.5_spmd} | conditional | flops 277944576 | bytes 10474604 | solution.py:44
  220.0 8.8 %conditional.2 = ((f32[8,1,256]{2,0,1:T(8,128)S(1)}, f32[8,1,256]{2,0,1:T(8,128)}, f32[8,1,256,128]{3,2,0,1:T(8,128)S(1)})) conditional(s32[]{:T(128)} %convert_element_type.119, (f32[8,1,256]{2,0,1:T(8,128)S(1)}, f32[8,1,256]{2,0,1:T(8,128)}, f32[8,1,256,128]{3,2,0,1:T(8,128)S(1)}) %tuple.51, (s32[]{:T(128)}, s32[256]{0:T(256)S(1)}, s32[256]{0:T(256)}, ...), branch_computations={%region_2.0_spmd, %region_3.5_spmd} | conditional | flops 277944576 | bytes 10474604 | solution.py:44
  233.5 8.8 %conditional.2 = ((f32[8,1,256]{2,0,1:T(8,128)S(1)}, f32[8,1,256]{2,0,1:T(8,128)}, f32[8,1,256,128]{3,2,0,1:T(8,128)S(1)})) conditional(s32[]{:T(128)} %convert_element_type.119, (f32[8,1,256]{2,0,1:T(8,128)S(1)}, f32[8,1,256]{2,0,1:T(8,128)}, f32[8,1,256,128]{3,2,0,1:T(8,128)S(1)}) %tuple.51, (s32[]{:T(128)}, s32[256]{0:T(256)S(1)}, s32[256]{0:T(256)}, ...), branch_computations={%region_2.0_spmd, %region_3.5_spmd} | conditional | flops 277944576 | bytes 10474604 | solution.py:44
  247.0 8.8 %conditional.2 = ((f32[8,1,256]{2,0,1:T(8,128)S(1)}, f32[8,1,256]{2,0,1:T(8,128)}, f32[8,1,256,128]{3,2,0,1:T(8,128)S(1)})) conditional(s32[]{:T(128)} %convert_element_type.119, (f32[8,1,256]{2,0,1:T(8,128)S(1)}, f32[8,1,256]{2,0,1:T(8,128)}, f32[8,1,256,128]{3,2,0,1:T(8,128)S(1)}) %tuple.51, (s32[]{:T(128)}, s32[256]{0:T(256)S(1)}, s32[256]{0:T(256)}, ...), branch_computations={%region_2.0_spmd, %region_3.5_spmd} | conditional | flops 277944576 | bytes 10474604 | solution.py:44
  260.5 8.8 %conditional.2 = ((f32[8,1,256]{2,0,1:T(8,128)S(1)}, f32[8,1,256]{2,0,1:T(8,128)}, f32[8,1,256,128]{3,2,0,1:T(8,128)S(1)})) conditional(s32[]{:T(128)} %convert_element_type.119, (f32[8,1,256]{2,0,1:T(8,128)S(1)}, f32[8,1,256]{2,0,1:T(8,128)}, f32[8,1,256,128]{3,2,0,1:T(8,128)S(1)}) %tuple.51, (s32[]{:T(128)}, s32[256]{0:T(256)S(1)}, s32[256]{0:T(256)}, ...), branch_computations={%region_2.0_spmd, %region_3.5_spmd} | conditional | flops 277944576 | bytes 10474604 | solution.py:44
  290.6 8.4 %all-to-all-start = ((bf16[8,256,128]{2,0,1:T(8,128)(2,1)}), bf16[8,256,128]{2,0,1:T(8,128)(2,1)S(1)}, u32[]{:S(2)}, u32[]{:S(2)}) async-start(bf16[8,256,128]{2,0,1:T(8,128)(2,1)} %fusion.38), calls=%async_computation | async-start | bytes 1048576 | tf_op jit(solution)/shard_map/all_to_all | solution.py:92
  299.3 18.0 %reduce-window.6 = s32[64,8,128]{2,1,0:T(8,128)S(1)} reduce-window(s32[64,8,128]{2,1,0:T(8,128)S(1)} %copy-done.2, s32[]{:T(128)} %constant.101.clone.1), window={size=1x1x128 pad=0_0x0_0x127_0}, to_apply=%region_10.11 | reduce-window | flops 8323072 | bytes 524292 | tf_op jit(solution)/shard_map/reduce-window
  323.5 13.1 %scatter_custom_fusion = bf16[2048,512]{1,0:T(8,128)(2,1)S(1)} fusion(s32[1024]{0:T(1024)S(1)} %bitcast.122, bf16[512,512]{1,0:T(8,128)(2,1)} %reshape.305, s32[1024]{0:T(1024)S(1)} %broadcast_clamp_fusion.1, bf16[]{:T(256)} %constant.114.clone.1), kind=kCustom, calls=%fused_computation.52 | custom fusion | bytes 2097664 | tf_op jit(solution)/shard_map/scatter | solution.py:121
  336.6 52.8 %all_to_all.42 = bf16[64,32,512]{2,1,0:T(8,128)(2,1)S(1)} all-to-all(bf16[64,32,512]{2,1,0:T(8,128)(2,1)S(1)} %bitcast.110), channel_id=1, replica_groups=mesh['seq'=16,'exp'=16] {'exp'}, dimensions={0} | all-to-all | bytes 4194304 | tf_op jit(solution)/shard_map/all_to_all | solution.py:124
  389.6 9.7 %fusion.31 = bf16[4,512,512]{2,1,0:T(8,128)(2,1)} fusion(bf16[4,1024,512]{2,1,0:T(8,128)(2,1)} %param.21, bf16[4,512,512]{2,1,0:T(8,128)(2,1)S(1)} %bitcast.114, bf16[4,512,1024]{2,1,0:T(8,128)(2,1)} %param.20), kind=kOutput, calls=%fused_computation.48 | convolution fusion | flops 4314890240 | bytes 12582912 | tf_op jit(solution)/shard_map/ecf,efs->ecs/dot_general | solution.py:129
  399.3 4.6 copy.159
  403.9 4.5 all-to-all-start.2
  410.5 8.6 %gather_fusion.1 = f32[1024]{0:T(1024)S(1)} fusion(f32[512,64]{0,1:T(8,128)S(1)} %fusion.54, s32[1024]{0:T(1024)S(1)} %reshape.331), kind=kCustom, calls=%fused_computation.2 | custom fusion | bytes 16384 | tf_op jit(solution)/shard_map/jit(take_along_axis)/gather | solution.py:106
  426.2 29.3 %all-to-all-done.2 = bf16[4,512,512]{2,0,1:T(4,128)(2,1)S(1)} async-done(((bf16[4,512,512]{2,0,1:T(4,128)(2,1)}), bf16[4,512,512]{2,0,1:T(4,128)(2,1)S(1)}, u32[]{:S(2)}, u32[]{:S(2)}) %all-to-all-start.2) | async-done | bytes 2097184 | tf_op jit(solution)/shard_map/all_to_all | solution.py:132
  459.1 4.0 gather_fusion
  (290 shorter events, 193.2 us)
Async XLA Ops:
  7.2 402.0 %copy-start = (bf16[512,64]{0,1:T(8,128)(2,1)S(1)}, bf16[512,64]{0,1:T(8,128)(2,1)}, u32[]{:S(2)}) copy-start(bf16[512,64]{0,1:T(8,128)(2,1)} %param.18) | copy-start | bytes 196612
  7.2 99.7 %all-gather.2.cloned.1.call-start = ((), (), s32[]{:S(2)}) async-start(), calls=%async_computation.3 | async-start | bytes 17825792 | tf_op jit(solution)/shard_map/all_gather | solution.py:75
  112.3 2.9 copy-start.3
  125.7 2.9 copy-start.3
  129.2 2.4 copy-start.4
  139.2 2.9 copy-start.3
  152.7 2.9 copy-start.3
  156.2 2.4 copy-start.4
  166.1 2.9 copy-start.3
  179.6 2.9 copy-start.3
  183.1 2.4 copy-start.4
  193.1 2.9 copy-start.3
  206.6 2.9 copy-start.3
  220.1 2.9 copy-start.3
  233.5 2.9 copy-start.3
  237.0 2.4 copy-start.4
  247.0 2.9 copy-start.3
  260.5 2.9 copy-start.3
  288.2 10.8 %copy-start.6 = (s32[16,8,4,2]{0,3,2,1:T(2,128)S(1)}, s32[16,8,4,2]{0,3,2,1:T(2,128)}, u32[]{:S(2)}) copy-start(s32[16,8,4,2]{0,3,2,1:T(2,128)} %param.19) | copy-start | bytes 12292
  288.2 11.0 %copy-start.8 = (f32[2048]{0:T(1024)S(1)}, f32[2048]{0:T(1024)}, u32[]{:S(2)}) copy-start(f32[2048]{0:T(1024)} %param.17) | copy-start | bytes 24580
  288.2 11.0 %copy-start.2 = (s32[64,8,128]{2,1,0:T(8,128)S(1)}, s32[64,8,128]{2,1,0:T(8,128)}, u32[]{:S(2)}) copy-start(s32[64,8,128]{2,1,0:T(8,128)} %fusion.43) | copy-start | bytes 786436
  290.6 28.0 %all-to-all-start = ((bf16[8,256,128]{2,0,1:T(8,128)(2,1)}), bf16[8,256,128]{2,0,1:T(8,128)(2,1)S(1)}, u32[]{:S(2)}, u32[]{:S(2)}) async-start(bf16[8,256,128]{2,0,1:T(8,128)(2,1)} %fusion.38), calls=%async_computation | async-start | bytes 1048576 | tf_op jit(solution)/shard_map/all_to_all | solution.py:92
  403.9 4.5 copy-start.7
  403.9 51.7 %all-to-all-start.2 = ((bf16[4,512,512]{2,0,1:T(4,128)(2,1)}), bf16[4,512,512]{2,0,1:T(4,128)(2,1)S(1)}, u32[]{:S(2)}, u32[]{:S(2)}) async-start(bf16[4,512,512]{2,0,1:T(4,128)(2,1)} %copy.159), calls=%async_computation.2 | async-start | bytes 4194304 | tf_op jit(solution)/shard_map/all_to_all | solution.py:132
  (10 other events, 23.2 us)
Sparse Core Ops, SparseCore 0:
  9.8 97.0 all-gather.1
where the time goes:
time: 481 us; the launch traced here: 476 us
  waiting for transfers between devices  123 us (26%)
  other arithmetic  101 us (21%)
  local copies, waits for them, and re-layouts  84.8 us (18%)
  matrix products  65 us (14%)
  blocking collectives  52.8 us (11%)
  loops' own time  21.3 us (4%)
  between operations  14.4 us (3%)
  starting transfers between devices  12.9 us (3%)
    all_gather x1, waiting for transfers between devices, body(): shard_part = lax.all_gather(stacked, 'seq', axis=2, tiled=True)  94.1 us
    all_to_all x1, blocking collectives, body(): lax.all_to_all(outgoing, 'exp', split_axis=0, concat_axis=1, tiled=True)  52.8 us
    all_to_all x1, waiting for transfers between devices, body(): lax.all_to_all(results, 'exp', split_axis=1, concat_axis=0, tiled=True)  29.3 us
    dot_general x12, matrix products, update(): jnp.einsum('bhqk,bkhd->bhqd', rounded_result, shaped[1], preferred_elemen...  29.1 us
    dot_general x12, matrix products, update(): jnp.einsum('bqhd,bkhd->bhqk', query_heads, shaped[0], preferred_element_t...  24.8 us
    reduce_or x16, other arithmetic, attend_block(): jnp.any(key_seg[:, -1] >= query_seg[:, 0])  22.3 us
    slice x16, local copies, waits for them, and re-layouts, attend_block(): query_pos[-1]  21.3 us
    another operation x1, loops' own time, body(): running = lax.fori_loop(0, repeats, inner, initial)  20.2 us
  transfers between devices with their start and end apart: 3, of which 2 were waited for; matrix products, arithmetic and copies ran while one was open for 9% of the time, Pallas kernels for 0%

commit v1 on v0

v1 whole, which is shorter than its diff:
```python
import functools

import jax
import jax.numpy as jnp
from jax import lax
from jax.experimental import pallas as pl
from jax.experimental.pallas import tpu as pltpu
from jax.sharding import PartitionSpec as P

HD = 128
SUB = 512
CAP = 32
NEG = -1e30
LOG2E = 1.4426950408889634

NS = 16
NE = 16
SEQS = 8
BLK = 256
HALF = 128
EPD = 4
ROWS = EPD * CAP
FFH = 1024
TOK = 16


def other(seq, exp):
    return {"seq": seq, "exp": exp}


def spread_kernel(q_ref, k_ref, v_ref, qo, ko, vo, loc, ksend, vsend, qsend, krecv, vrecv, qrecv, kfwd, vfwd):
    s = lax.axis_index("seq")
    e = lax.axis_index("exp")
    c = s // 2
    k = s % 2
    partner = 2 * c + 1 - k

    barrier = pltpu.get_barrier_semaphore()

    def greet(i, _):
        pl.semaphore_signal(barrier, inc=1, device_id=other((s + i) % NS, e), device_id_type=pl.DeviceIdType.MESH)
        return 0

    lax.fori_loop(1, NS, greet, 0)
    pl.semaphore_wait(barrier, NS - 1)

    def remote(src, dst, ss, rs, seq):
        return pltpu.make_async_remote_copy(
            src_ref=src, dst_ref=dst, send_sem=ss, recv_sem=rs,
            device_id=other(seq, e), device_id_type=pl.DeviceIdType.MESH,
        )

    def sends(j):
        b = (c + j) % SEQS
        same = 2 * b + k
        cross = 2 * b + 1 - k
        return (
            remote(k_ref.at[b], ko.at[s], ksend.at[j], krecv.at[s], same),
            remote(v_ref.at[b], vo.at[s], vsend.at[j], vrecv.at[s], same),
            remote(q_ref.at[b, k], qo.at[s], qsend.at[j], qrecv.at[s], same),
            remote(q_ref.at[b, 1 - k], qo.at[s], qsend.at[SEQS + j], qrecv.at[s], cross),
        )

    def start(j, _):
        for copy in sends(j):
            copy.start()
        return 0

    lax.fori_loop(1, SEQS, start, 0)

    own = (
        pltpu.make_async_copy(k_ref.at[c], ko.at[s], loc.at[0]),
        pltpu.make_async_copy(v_ref.at[c], vo.at[s], loc.at[1]),
        pltpu.make_async_copy(q_ref.at[c, k], qo.at[s], loc.at[2]),
    )
    near = (
        remote(k_ref.at[c], ko.at[s], kfwd.at[0], krecv.at[s], partner),
        remote(v_ref.at[c], vo.at[s], vfwd.at[0], vrecv.at[s], partner),
        remote(q_ref.at[c, 1 - k], qo.at[s], qsend.at[0], qrecv.at[s], partner),
    )
    for copy in own + near:
        copy.start()

    def forward(j):
        src = 2 * ((c + SEQS - j) % SEQS) + k
        return (
            remote(ko.at[src], ko.at[src], kfwd.at[j], krecv.at[src], partner),
            remote(vo.at[src], vo.at[src], vfwd.at[j], vrecv.at[src], partner),
        )

    def relay(j, _):
        for copy in forward(j):
            copy.wait_recv()
            copy.start()
        return 0

    lax.fori_loop(1, SEQS, relay, 0)

    def finish(j, _):
        src = 2 * ((c + SEQS - j) % SEQS) + 1 - k
        remote(ko.at[src], ko.at[src], kfwd.at[j], krecv.at[src], partner).wait_recv()
        remote(vo.at[src], vo.at[src], vfwd.at[j], vrecv.at[src], partner).wait_recv()
        return 0

    lax.fori_loop(0, SEQS, finish, 0)

    def finish_q(i, _):
        src = (s + i) % NS
        remote(qo.at[src], qo.at[src], qsend.at[0], qrecv.at[src], partner).wait_recv()
        return 0

    lax.fori_loop(1, NS, finish_q, 0)

    def drain(j, _):
        for copy in sends(j) + forward(j):
            copy.wait_send()
        return 0

    lax.fori_loop(1, SEQS, drain, 0)
    for copy in own:
        copy.wait()
    for copy in near:
        copy.wait_send()


def spread(queries, keys, values):
    hbm = pl.BlockSpec(memory_space=pl.ANY)
    dma = pltpu.SemaphoreType.DMA
    return pl.pallas_call(
        spread_kernel,
        out_shape=(
            jax.ShapeDtypeStruct((NS, HALF, HD), jnp.bfloat16),
            jax.ShapeDtypeStruct((NS, BLK, HD), jnp.bfloat16),
            jax.ShapeDtypeStruct((NS, BLK, HD), jnp.bfloat16),
        ),
        in_specs=[hbm] * 3,
        out_specs=(hbm, hbm, hbm),
        scratch_shapes=[
            dma((3,)), dma((SEQS,)), dma((SEQS,)), dma((2 * SEQS,)),
            dma((NS,)), dma((NS,)), dma((NS,)), dma((SEQS,)), dma((SEQS,)),
        ],
        compiler_params=pltpu.CompilerParams(collective_id=0, has_side_effects=True),
        name="spread",
    )(queries.reshape(SEQS, 2, HALF, HD), keys, values)


QG = 256
KC = 512
GROUPS = 8


def attention_kernel(seg_ref, q_ref, k_ref, v_ref, o_ref, mx_ref, sum_ref, acc_ref):
    s = lax.axis_index("seq")
    c = s // 2
    k = s % 2
    seg = seg_ref[pl.ds(c, 1), :]
    firsts = [jnp.sum((seg < v).astype(jnp.int32)) for v in (1, 2, 3)]
    scale = HD ** (-0.5) * LOG2E

    for m in range(GROUPS):
        first_pos = m * KC + k * HALF
        lowest = 0
        for f in firsts:
            lowest = jnp.where(f <= first_pos, f, lowest)
        mx_ref[...] = jnp.full((QG, HD), NEG, jnp.float32)
        sum_ref[...] = jnp.zeros((QG, HD), jnp.float32)
        acc_ref[...] = jnp.zeros((QG, HD), jnp.float32)

        def chunk(j, _):
            kk = k_ref[pl.ds(2 * j, 2)].reshape(KC, HD)
            vv = v_ref[pl.ds(2 * j, 2)].reshape(KC, HD)
            base = j * KC
            for half in range(2):
                rows = pl.ds(half * HALF, HALF)
                qq = q_ref[2 * m + half]
                scores = lax.dot_general(qq, kk, (((1,), (1,)), ((), ())), preferred_element_type=jnp.float32)
                pos = lax.broadcasted_iota(jnp.int32, (HALF, 1), 0) + (first_pos + half * BLK)
                begin = jnp.zeros((HALF, 1), jnp.int32)
                for f in firsts:
                    begin = jnp.where(pos >= f, f, begin)
                key_pos = lax.broadcasted_iota(jnp.int32, (HALF, KC), 1)
                scores = jnp.where((key_pos <= pos - base) & (key_pos >= begin - base), scores, NEG)
                old = mx_ref[rows, 0:1]
                new = jnp.maximum(old, jnp.max(scores, axis=-1, keepdims=True))
                weights = jnp.exp2((scores - new) * scale)
                factor = jnp.exp2((old - new) * scale)
                part = weights[:, 0:HD]
                for i in range(1, KC // HD):
                    part = part + weights[:, i * HD:(i + 1) * HD]
                sum_ref[rows, :] = sum_ref[rows, :] * factor + part
                acc_ref[rows, :] = acc_ref[rows, :] * factor + jnp.dot(
                    weights.astype(jnp.bfloat16), vv, preferred_element_type=jnp.float32
                )
                mx_ref[rows, :] = jnp.broadcast_to(new, (HALF, HD))
            return 0

        lax.fori_loop(lowest // KC, m + 1, chunk, 0)
        total = jnp.sum(sum_ref[...], axis=-1, keepdims=True)
        o_ref[2 * m:2 * m + 2] = (acc_ref[...] / total).astype(jnp.bfloat16).reshape(2, HALF, HD)


def attention(seg_ids, q, k, v):
    vmem = pl.BlockSpec(memory_space=pltpu.VMEM)
    return pl.pallas_call(
        attention_kernel,
        out_shape=jax.ShapeDtypeStruct((NS, HALF, HD), jnp.bfloat16),
        in_specs=[vmem] * 4,
        out_specs=vmem,
        scratch_shapes=[pltpu.VMEM((QG, HD), jnp.float32)] * 3,
        name="attention",
    )(seg_ids, q, k, v)


def moe_kernel(
    o_ref, ids_ref, gain_ref, rw_ref, win_hbm, wout_hbm, normed_ref, mix_ref,
    tok, xbuf, outbuf, arrived, res, returned, win, wout, acc, cols, spare,
    wsem, osend, orecv, dsend, drecv, rsend, rrecv,
):
    s = lax.axis_index("seq")
    e = lax.axis_index("exp")
    c = s // 2
    k = s % 2
    f32, bf16 = jnp.float32, jnp.bfloat16
    mesh_id = pl.DeviceIdType.MESH

    loads = (
        pltpu.make_async_copy(win_hbm, win, wsem.at[0]),
        pltpu.make_async_copy(wout_hbm, wout, wsem.at[1]),
    )
    for copy in loads:
        copy.start()

    barrier = pltpu.get_barrier_semaphore()
    number = s * NE + e

    def greet(i, _):
        t = (number + i) % (NS * NE)
        pl.semaphore_signal(barrier, inc=1, device_id=other(t // NE, t % NE), device_id_type=mesh_id)
        return 0

    lax.fori_loop(1, NS * NE, greet, 0)
    pl.semaphore_wait(barrier, NS * NE - 1)

    def give(i, _):
        sp = (s + i // 8) % NS
        ei = (e + i) % 8
        ep = k * 8 + ei
        mine = (sp == s) & (ep == e)

        @pl.when(jnp.logical_not(mine))
        def _():
            pltpu.make_async_remote_copy(
                src_ref=o_ref.at[sp, ei], dst_ref=tok.at[c, e], send_sem=osend, recv_sem=orecv.at[c],
                device_id=other(sp, ep), device_id_type=mesh_id,
            ).start()

        @pl.when(mine)
        def _():
            pltpu.make_async_copy(o_ref.at[sp, ei], tok.at[c, e], orecv.at[c]).start()
            pltpu.make_async_copy(o_ref.at[sp, ei], spare, osend).start()

        return 0

    lax.fori_loop(0, 8 * NS, give, 0)

    ids = ids_ref[...]
    experts = lax.broadcasted_iota(jnp.int32, (64, SUB), 0)
    before = (
        lax.broadcasted_iota(jnp.int32, (SUB, SUB), 0) < lax.broadcasted_iota(jnp.int32, (SUB, SUB), 1)
    ).astype(f32).astype(bf16)
    hot0 = (experts == ids[0:1]).astype(f32)
    hot1 = (experts == ids[1:2]).astype(f32)
    run0 = jnp.dot(hot0.astype(bf16), before, preferred_element_type=f32)
    run1 = jnp.dot(hot1.astype(bf16), before, preferred_element_type=f32)
    run1 = run1 + jnp.sum(hot0, axis=1, keepdims=True)
    idf = ids.astype(f32)
    slot0 = idf[0:1] * CAP + jnp.sum(run0 * hot0, axis=0, keepdims=True)
    slot1 = idf[1:2] * CAP + jnp.sum(run1 * hot1, axis=0, keepdims=True)
    lines = jnp.concatenate([slot0, slot1, idf, jnp.zeros((124, SUB), f32)], axis=0)
    lines = jnp.transpose(lines)
    cols[0] = jnp.broadcast_to(lines[:, 0:1], (SUB, HD))
    cols[1] = jnp.broadcast_to(lines[:, 1:2], (SUB, HD))
    lanes64 = lax.broadcasted_iota(jnp.int32, (SUB, 64), 1).astype(f32)
    pick0 = lanes64 == lines[:, 2:3]
    pick1 = lanes64 == lines[:, 3:4]

    gain = gain_ref[...]

    def norm(b, _):
        pltpu.make_async_copy(tok.at[b], tok.at[b], orecv.at[b]).wait()
        v = tok[b].astype(f32)
        square = jnp.sum(jnp.sum(v * v, axis=0), axis=-1, keepdims=True)
        spread_ = jnp.sqrt(square * (1.0 / 2048.0) + 1e-6)
        n = (v / spread_[None] * gain[:, None, :]).astype(bf16)
        for h in range(16):
            normed_ref[b, :, h * HD:(h + 1) * HD] = n[h]
            xbuf[b * 4 + h // 4, :, (h % 4) * HD:(h % 4 + 1) * HD] = n[h]
        return 0

    lax.fori_loop(0, SEQS, norm, 0)

    x = xbuf[...].reshape(SUB, SUB)

    def sending(i):
        d = (e + i) % NE
        return pltpu.make_async_remote_copy(
            src_ref=outbuf.at[i], dst_ref=arrived.at[e], send_sem=dsend.at[i], recv_sem=drecv.at[e],
            device_id=other(s, d), device_id_type=mesh_id,
        )

    slot_line = lax.broadcasted_iota(jnp.int32, (ROWS, SUB), 0)

    def gathered(i):
        d = (e + i) % NE
        slot = (slot_line + d * ROWS).astype(f32)
        chosen = ((slot == slot0) | (slot == slot1)).astype(f32).astype(bf16)
        rows = jnp.dot(chosen, xbuf[...].reshape(SUB, SUB), preferred_element_type=f32)
        return rows.astype(bf16).reshape(EPD, CAP, SUB)

    def dispatch(i, _):
        outbuf[i] = gathered(i)
        sending(i).start()
        return 0

    lax.fori_loop(1, NE, dispatch, 0)
    arrived[e] = gathered(0)

    logits = jnp.dot(x, rw_ref[...], preferred_element_type=f32)
    sig0 = 1.0 / (1.0 + jnp.exp(-jnp.sum(jnp.where(pick0, logits, 0.0), axis=1, keepdims=True)))
    sig1 = 1.0 / (1.0 + jnp.exp(-jnp.sum(jnp.where(pick1, logits, 0.0), axis=1, keepdims=True)))
    cols[2] = jnp.broadcast_to(sig0 / (sig0 + sig1), (SUB, HD))
    cols[3] = jnp.broadcast_to(sig1 / (sig0 + sig1), (SUB, HD))
    acc[...] = jnp.zeros((SUB, SUB), f32)

    for copy in loads:
        copy.wait()

    def giving(i):
        src = (e + NE - i) % NE
        return pltpu.make_async_remote_copy(
            src_ref=res.at[i], dst_ref=returned.at[e], send_sem=rsend.at[i], recv_sem=rrecv.at[e],
            device_id=other(s, src), device_id_type=mesh_id,
        )

    def group(q, _):
        sources = [(e + NE - (q * 4 + j)) % NE for j in range(4)]
        for j in range(4):
            src = sources[j]

            @pl.when(src != e)
            def _():
                pltpu.make_async_copy(arrived.at[src], arrived.at[src], drecv.at[src]).wait()

        def one(xp, _):
            a = jnp.concatenate([arrived[src, xp] for src in sources], axis=0)
            u = jnp.dot(a, win[xp], preferred_element_type=f32)
            hid = 0.5 * u * (1.0 + jnp.tanh(0.7978845608028654 * (u + 0.044715 * (u * u * u))))
            y = jnp.dot(hid.astype(bf16), wout[xp], preferred_element_type=f32).astype(bf16)
            for j in range(4):
                res[q * 4 + j, xp] = y[j * CAP:(j + 1) * CAP]
            return 0

        lax.fori_loop(0, EPD, one, 0)
        for j in range(4):
            i = q * 4 + j

            @pl.when(i != 0)
            def _():
                giving(i).start()

        return 0

    lax.fori_loop(0, 4, group, 0)
    returned[e] = res[0]

    lane = lax.broadcasted_iota(jnp.int32, (SUB, HD), 1)

    def combine(p, _):
        parts = []
        tables = []
        for j in range(2):
            d = (e + 2 * p + j) % NE

            @pl.when(d != e)
            def _():
                pltpu.make_async_copy(returned.at[d], returned.at[d], rrecv.at[d]).wait()

            slot = (lane + d * ROWS).astype(f32)
            tables.append(
                jnp.where(slot == cols[0], cols[2], 0.0) + jnp.where(slot == cols[1], cols[3], 0.0)
            )
            parts.append(returned[d].reshape(ROWS, SUB))
        table = jnp.concatenate(tables, axis=1)
        rows = jnp.concatenate(parts, axis=0)
        high = table.astype(bf16)
        low = (table - high.astype(f32)).astype(bf16)
        acc[...] += jnp.dot(high, rows, preferred_element_type=f32) + jnp.dot(low, rows, preferred_element_type=f32)
        return 0

    lax.fori_loop(0, NE // 2, combine, 0)
    for b in range(SEQS):
        for g in range(4):
            mix_ref[b, :, g * SUB:(g + 1) * SUB] = acc[(b * 4 + g) * TOK:(b * 4 + g + 1) * TOK].astype(bf16)

    pltpu.make_async_copy(o_ref, o_ref, osend).wait()

    def drain(i, _):
        sending(i).wait_send()
        giving(i).wait_send()
        return 0

    lax.fori_loop(1, NE, drain, 0)


def moe(o, ids, gain, router_w, w_in, w_out):
    vmem = pl.BlockSpec(memory_space=pltpu.VMEM)
    hbm = pl.BlockSpec(memory_space=pl.ANY)
    dma = pltpu.SemaphoreType.DMA
    bf16, f32 = jnp.bfloat16, jnp.float32
    return pl.pallas_call(
        moe_kernel,
        out_shape=(
            jax.ShapeDtypeStruct((SEQS, TOK, 2048), bf16),
            jax.ShapeDtypeStruct((SEQS, TOK, 2048), bf16),
        ),
        in_specs=[vmem] * 4 + [hbm] * 2,
        out_specs=(vmem, vmem),
        scratch_shapes=[
            pltpu.VMEM((SEQS, NE, TOK, HD), bf16),
            pltpu.VMEM((32, TOK, SUB), bf16),
            pltpu.VMEM((NE, EPD, CAP, SUB), bf16),
            pltpu.VMEM((NE, EPD, CAP, SUB), bf16),
            pltpu.VMEM((NE, EPD, CAP, SUB), bf16),
            pltpu.VMEM((NE, EPD, CAP, SUB), bf16),
            pltpu.VMEM((EPD, SUB, FFH), bf16),
            pltpu.VMEM((EPD, FFH, SUB), bf16),
            pltpu.VMEM((SUB, SUB), f32),
            pltpu.VMEM((4, SUB, HD), f32),
            pltpu.VMEM((TOK, HD), bf16),
            dma((2,)), dma(()), dma((SEQS,)), dma((NE,)), dma((NE,)), dma((NE,)), dma((NE,)),
        ],
        compiler_params=pltpu.CompilerParams(
            collective_id=1, has_side_effects=True, vmem_limit_bytes=56 * 1024 * 1024
        ),
        name="moe",
    )(o, ids, gain, router_w, w_in, w_out)


def body(queries, keys, values, seg_ids, norm_gain, router_w, expert_ids, w_in, w_out):
    q, k, v = spread(queries, keys, values)
    o = attention(seg_ids, q, k, v)
    ids = expert_ids.transpose(3, 1, 2, 0).reshape(2, SUB)
    return moe(
        o.reshape(NS, 8, TOK, HD), ids, norm_gain.reshape(16, HD), router_w, w_in, w_out
    )


def solution(mesh):
    return jax.shard_map(
        body,
        mesh=mesh,
        in_specs=(
            P(None, "seq", "exp"),
            P(None, "seq", "exp"),
            P(None, "seq", "exp"),
            P(),
            P(),
            P(),
            P(("seq", "exp"), None, None, None),
            P("exp", None, None),
            P("exp", None, None),
        ),
        out_specs=(P(None, ("seq", "exp"), None), P(None, ("seq", "exp"), None)),
        check_vma=False,
    )
```

time: 481 us -> 195 us (0.41)
  the two profiles are of different devices: /device:TPU:13 before, /device:TPU:120 now
where the time goes in v1:
time: 195 us
  Pallas kernels  189 us (97%)
  local copies, waits for them, and re-layouts  5.22 us (3%)
    pallas_call x1, Pallas kernels, moe(): pl.pallas_call(moe_kernel, out_shape=(jax.ShapeDtypeStruct((SEQS, TOK, 20...  137 us
    pallas_call x1, Pallas kernels, spread(): pl.pallas_call(spread_kernel, out_shape=(jax.ShapeDtypeStruct((NS, HALF,...  29.4 us
    pallas_call x1, Pallas kernels, attention(): pl.pallas_call(attention_kernel, out_shape=jax.ShapeDtypeStruct((NS, HALF...  22.7 us
    unnamed x7, local copies, waits for them, and re-layouts  4.53 us

profile of v1, /device:TPU:120, one launch (start us, length us, event | category | flops | bytes accessed | tf_op | source)
XLA Modules:
  0.0 194.6 jit_solution(16403392760724395743)
XLA Ops:
  0.6 0.0 copy-start
  0.6 0.0 copy-start.1
  0.7 29.4 %spread.1 = (bf16[16,128,128]{2,1,0:T(8,128)(2,1)}, bf16[16,256,128]{2,1,0:T(8,128)(2,1)}, bf16[16,256,128]{2,1,0:T(8,128)(2,1)}) custom-call(bf16[8,2,128,128]{3,2,1,0:T(8,128)(2,1)} %bitcast.5, bf16[8,256,128]{2,1,0:T(8,128)(2,1)} %k_ref.1, bf16[8,256,128]{2,1,0:T(8,128)(2,1)} %v_ref.1), custom_call_target="tpu_custom_call" | custom-call | tf_op jit(solution)/shard_map/spread/pallas_call | solution.py:129
  30.1 22.7 %attention.1 = bf16[16,128,128]{2,1,0:T(8,128)(2,1)} custom-call(s32[8,4096]{1,0:T(8,128)} %seg_ref.1, bf16[16,128,128]{2,1,0:T(8,128)(2,1)} %get-tuple-element.5.q_ref, bf16[16,256,128]{2,1,0:T(8,128)(2,1)} %get-tuple-element.6.k_ref, bf16[16,256,128]{2,1,0:T(8,128)(2,1)} %get-tuple-element.7.v_ref), custom_call_target="tpu_custom_call" | custom-call | tf_op jit(solution)/shard_map/attention/pallas_call | solution.py:204
  52.8 0.0 copy-done
  52.8 0.8 copy.12.rw_ref
  53.5 0.0 copy-done.1
  53.6 0.7 reshape.18.ids_ref
  54.2 136.6 %moe.1 = (bf16[8,16,2048]{2,1,0:T(8,128)(2,1)}, bf16[8,16,2048]{2,1,0:T(8,128)(2,1)}) custom-call(bf16[16,8,16,128]{3,2,1,0:T(8,128)(2,1)} %bitcast.4, s32[2,512]{1,0:T(2,128)} %reshape.18.ids_ref, f32[16,128]{1,0:T(8,128)} %bitcast.7, bf16[512,64]{1,0:T(8,128)(2,1)} %copy.12.rw_ref, bf16[4,512,1024]{2,1,0:T(8,128)(2,1)} %win_hbm.1, ...), custom_call_target="tpu_custom_call" | custom-call | tf_op jit(solution)/shard_map/moe/pallas_call | solution.py:420
  190.9 1.9 copy.15
  192.8 1.9 copy.16
  (1 shorter events, 0.0 us)
Async XLA Ops:
  0.6 52.2 %copy-start = (bf16[512,64]{0,1:T(8,128)(2,1)S(1)}, bf16[512,64]{0,1:T(8,128)(2,1)}, u32[]{:S(2)}) copy-start(bf16[512,64]{0,1:T(8,128)(2,1)} %param.14) | copy-start | bytes 196612
  0.6 52.9 %copy-start.1 = (s32[16,8,4,2]{0,3,2,1:T(2,128)S(1)}, s32[16,8,4,2]{0,3,2,1:T(2,128)}, u32[]{:S(2)}) copy-start(s32[16,8,4,2]{0,3,2,1:T(2,128)} %param.15) | copy-start | bytes 12292

commit v2 on v1

v2 whole, which is shorter than its diff:
```python
import functools

import jax
import jax.numpy as jnp
from jax import lax
from jax.experimental import pallas as pl
from jax.experimental.pallas import tpu as pltpu
from jax.sharding import PartitionSpec as P

HD = 128
SUB = 512
CAP = 32
NEG = -1e30
LOG2E = 1.4426950408889634

NS = 16
NE = 16
SEQS = 8
BLK = 256
HALF = 128
EPD = 4
ROWS = EPD * CAP
FFH = 1024
TOK = 16

QG = 256
KC = 512
GROUPS = 8
BIG = 2.0**100
MESH = pl.DeviceIdType.MESH


def other(seq, exp):
    return {"seq": seq, "exp": exp}


def offset_of(i):
    p = i // 2
    mag = 4 - (p + 1) // 2
    return (i + 1) % 2, jnp.where(p % 2 == 0, NZ - mag, mag)


NZ = 8


def partner_to(e, i):
    dy, dz = offset_of(i)
    return (e // NZ + dy) % 2 * NZ + (e % NZ + dz) % NZ


def partner_from(e, i):
    dy, dz = offset_of(i)
    return (e // NZ + dy) % 2 * NZ + (e % NZ + NZ - dz) % NZ


def kernel(
    q_ref, k_ref, v_ref, seg_ref, ids_ref, gain_ref, rw_ref, win_hbm, wout_hbm, normed_ref, mix_ref,
    qbuf, kbuf, vbuf, qaug, kaug, sbuf, pmax, mrow, asum, aacc, obuf,
    tok, xbuf, outbuf, arrived, res, returned, win, wout, acc, cols, spare,
    ready, loc, ksend, vsend, qsend, krecv, vrecv, qrecv, kfwd, vfwd,
    wsem, osend, orecv, dsend, drecv, rsend, rrecv,
):
    s = lax.axis_index("seq")
    e = lax.axis_index("exp")
    c = s // 2
    k = s % 2
    other_core = 2 * c + 1 - k
    f32, bf16 = jnp.float32, jnp.bfloat16

    loads = (
        pltpu.make_async_copy(win_hbm, win, wsem.at[0]),
        pltpu.make_async_copy(wout_hbm, wout, wsem.at[1]),
    )

    barrier = pltpu.get_barrier_semaphore()

    def greet(i, _):
        pl.semaphore_signal(barrier, inc=1, device_id=other((s + i) % NS, e), device_id_type=MESH)
        pl.semaphore_signal(barrier, inc=1, device_id=other(s, (e + i) % NE), device_id_type=MESH)
        return 0

    lax.fori_loop(1, NS, greet, 0)
    pl.semaphore_wait(barrier, 2 * (NS - 1))

    def remote(src, dst, ss, rs, seq, exp):
        return pltpu.make_async_remote_copy(
            src_ref=src, dst_ref=dst, send_sem=ss, recv_sem=rs, device_id=other(seq, exp), device_id_type=MESH
        )

    def sends(j):
        b = (c + j) % SEQS
        same = 2 * b + k
        cross = 2 * b + 1 - k
        return (
            remote(k_ref.at[b], kbuf.at[s], ksend.at[j], krecv.at[s], same, e),
            remote(v_ref.at[b], vbuf.at[s], vsend.at[j], vrecv.at[s], same, e),
            remote(q_ref.at[b, k], qbuf.at[s], qsend.at[j], qrecv.at[s], same, e),
            remote(q_ref.at[b, 1 - k], qbuf.at[s], qsend.at[SEQS + j], qrecv.at[s], cross, e),
        )

    def start(j, _):
        for copy in sends(j):
            copy.start()
        return 0

    lax.fori_loop(1, SEQS, start, 0)
    own = (
        pltpu.make_async_copy(k_ref.at[c], kbuf.at[s], loc.at[0]),
        pltpu.make_async_copy(v_ref.at[c], vbuf.at[s], loc.at[1]),
        pltpu.make_async_copy(q_ref.at[c, k], qbuf.at[s], loc.at[2]),
    )
    near = (
        remote(k_ref.at[c], kbuf.at[s], kfwd.at[0], krecv.at[s], other_core, e),
        remote(v_ref.at[c], vbuf.at[s], vfwd.at[0], vrecv.at[s], other_core, e),
        remote(q_ref.at[c, 1 - k], qbuf.at[s], qsend.at[0], qrecv.at[s], other_core, e),
    )
    for copy in own + near + loads:
        copy.start()

    def greet_again(i, _):
        pl.semaphore_signal(ready, inc=1, device_id=other(s, (e + i) % NE), device_id_type=MESH)
        return 0

    lax.fori_loop(1, NE, greet_again, 0)

    seg = seg_ref[pl.ds(c, 1), :]
    firsts = [jnp.sum((seg < v).astype(jnp.int32)) for v in (1, 2, 3)]

    def document(pos):
        return sum((pos >= f).astype(jnp.int32) for f in firsts)

    def mark(j, _):
        key_pos = lax.broadcasted_iota(jnp.int32, (KC, HD), 0) + j * KC
        lane = lax.broadcasted_iota(jnp.int32, (KC, HD), 1)
        kaug[j] = (document(key_pos) == lane).astype(f32).astype(bf16)
        row = lax.broadcasted_iota(jnp.int32, (QG, HD), 0)
        query_pos = row + jnp.where(row >= HALF, HALF, 0) + (j * KC + k * HALF)
        lane = lax.broadcasted_iota(jnp.int32, (QG, HD), 1)
        qaug[j] = jnp.where(document(query_pos) == lane, 0.0, -BIG).astype(bf16)
        return 0

    lax.fori_loop(0, GROUPS, mark, 0)

    ids = ids_ref[...]
    experts = lax.broadcasted_iota(jnp.int32, (64, SUB), 0)
    before = (
        lax.broadcasted_iota(jnp.int32, (SUB, SUB), 0) < lax.broadcasted_iota(jnp.int32, (SUB, SUB), 1)
    ).astype(f32).astype(bf16)
    hot0 = (experts == ids[0:1]).astype(f32)
    hot1 = (experts == ids[1:2]).astype(f32)
    run0 = jnp.dot(hot0.astype(bf16), before, preferred_element_type=f32)
    run1 = jnp.dot(hot1.astype(bf16), before, preferred_element_type=f32)
    run1 = run1 + jnp.sum(hot0, axis=1, keepdims=True)
    idf = ids.astype(f32)
    slot0 = idf[0:1] * CAP + jnp.sum(run0 * hot0, axis=0, keepdims=True)
    slot1 = idf[1:2] * CAP + jnp.sum(run1 * hot1, axis=0, keepdims=True)
    lines = jnp.concatenate([slot0, slot1, idf, jnp.zeros((124, SUB), f32)], axis=0)
    lines = jnp.transpose(lines)
    for i in range(4):
        cols[i] = jnp.broadcast_to(lines[:, i:i + 1], (SUB, HD))

    def forward(j):
        src = 2 * ((c + SEQS - j) % SEQS) + k
        return (
            remote(kbuf.at[src], kbuf.at[src], kfwd.at[j], krecv.at[src], other_core, e),
            remote(vbuf.at[src], vbuf.at[src], vfwd.at[j], vrecv.at[src], other_core, e),
        )

    def relay(j, _):
        for copy in forward(j):
            copy.wait_recv()
            copy.start()
        return 0

    lax.fori_loop(1, SEQS, relay, 0)

    def finish(j, _):
        src = 2 * ((c + SEQS - j) % SEQS) + 1 - k
        pltpu.make_async_copy(kbuf.at[src], kbuf.at[src], krecv.at[src]).wait()
        pltpu.make_async_copy(vbuf.at[src], vbuf.at[src], vrecv.at[src]).wait()
        return 0

    lax.fori_loop(0, SEQS, finish, 0)

    def finish_q(i, _):
        src = (s + i) % NS
        pltpu.make_async_copy(qbuf.at[src], qbuf.at[src], qrecv.at[src]).wait()
        return 0

    lax.fori_loop(1, NS, finish_q, 0)
    for copy in own:
        copy.wait()
    pl.semaphore_wait(ready, NE - 1)

    scale = HD ** (-0.5) * LOG2E

    def scores_of(m, j):
        qq = jnp.concatenate([qbuf[pl.ds(2 * m, 2)].reshape(QG, HD), qaug[m]], axis=1)
        kk = jnp.concatenate([kbuf[pl.ds(2 * j, 2)].reshape(KC, HD), kaug[j]], axis=1)
        return lax.dot_general(qq, kk, (((1,), (1,)), ((), ())), preferred_element_type=f32)

    def tiles(x, op):
        out = x[:, 0:HD]
        for i in range(1, KC // HD):
            out = op(out, x[:, i * HD:(i + 1) * HD])
        return out

    def first_pass(m, j):
        scores = scores_of(m, j)
        sbuf[m % 2, j] = scores
        pmax[m % 2] = jnp.maximum(pmax[m % 2], tiles(scores, jnp.maximum))

    def diagonal(m):
        scores = scores_of(m, m)
        row = lax.broadcasted_iota(jnp.int32, (QG, KC), 0)
        row = row + jnp.where(row >= HALF, HALF, 0) + k * HALF
        scores = jnp.where(lax.broadcasted_iota(jnp.int32, (QG, KC), 1) <= row, scores, -BIG)
        sbuf[m % 2, m] = scores
        highest = jnp.maximum(pmax[m % 2], tiles(scores, jnp.maximum))
        mrow[...] = jnp.broadcast_to(jnp.max(highest, axis=-1, keepdims=True), (QG, HD))

    def second_pass(m, j):
        top = mrow[...]
        top = jnp.concatenate([top] * (KC // HD), axis=1)
        weights = jnp.exp2((sbuf[m % 2, j] - top) * scale)
        asum[...] += tiles(weights, jnp.add)
        vv = vbuf[pl.ds(2 * j, 2)].reshape(KC, HD)
        aacc[...] += jnp.dot(weights.astype(bf16), vv, preferred_element_type=f32)

    def clear(m):
        pmax[m % 2] = jnp.full((QG, HD), -BIG, f32)

    def only_first(j, _):
        first_pass(c, j)
        return 0

    clear(c)
    lax.fori_loop(0, c, only_first, 0)
    diagonal(c)

    def attend(t, _):
        m = (c + t) % GROUPS
        after = (m + 1) % GROUPS
        asum[...] = jnp.zeros((QG, HD), f32)
        aacc[...] = jnp.zeros((QG, HD), f32)
        clear(after)
        both = (m < GROUPS - 1) & (t < GROUPS - 1)

        @pl.when(both)
        def _():
            def step(j, _):
                first_pass(m + 1, j)
                second_pass(m, j)
                return 0

            lax.fori_loop(0, m + 1, step, 0)

        @pl.when(jnp.logical_not(both))
        def _():
            def step(j, _):
                second_pass(m, j)
                return 0

            lax.fori_loop(0, m + 1, step, 0)

        total = jnp.sum(asum[...], axis=-1, keepdims=True)
        obuf[pl.ds(2 * m, 2)] = (aacc[...] / total).astype(bf16).reshape(2, 8, TOK, HD)

        def give(i, _):
            sp = 2 * m + i // 8
            ei = (e + i) % 8
            ep = k * 8 + ei
            mine = (sp == s) & (ep == e)

            @pl.when(jnp.logical_not(mine))
            def _():
                remote(obuf.at[sp, ei], tok.at[c, e], osend, orecv.at[c], sp, ep).start()

            @pl.when(mine)
            def _():
                pltpu.make_async_copy(obuf.at[sp, ei], tok.at[c, e], orecv.at[c]).start()
                pltpu.make_async_copy(obuf.at[sp, ei], spare, osend).start()

            return 0

        lax.fori_loop(0, 16, give, 0)

        @pl.when(t < GROUPS - 1)
        def _():
            diagonal(after)

        return 0

    lax.fori_loop(0, GROUPS, attend, 0)

    gain = gain_ref[...]

    def norm(b, _):
        pltpu.make_async_copy(tok.at[b], tok.at[b], orecv.at[b]).wait()
        v = tok[b].astype(f32)
        square = jnp.sum(jnp.sum(v * v, axis=0), axis=-1, keepdims=True)
        spread = jnp.sqrt(square * (1.0 / 2048.0) + 1e-6)
        n = (v / spread[None] * gain[:, None, :]).astype(bf16)
        for h in range(16):
            normed_ref[b, :, h * HD:(h + 1) * HD] = n[h]
            xbuf[b * 4 + h // 4, :, (h % 4) * HD:(h % 4 + 1) * HD] = n[h]
        return 0

    lax.fori_loop(0, SEQS, norm, 0)

    def sending(i):
        return remote(outbuf.at[i], arrived.at[e], dsend.at[i], drecv.at[e], s, partner_to(e, i))

    slot_line = lax.broadcasted_iota(jnp.int32, (ROWS, SUB), 0)

    def gathered(d):
        slot = (slot_line + d * ROWS).astype(f32)
        chosen = ((slot == slot0) | (slot == slot1)).astype(f32).astype(bf16)
        rows = jnp.dot(chosen, xbuf[...].reshape(SUB, SUB), preferred_element_type=f32)
        return rows.astype(bf16).reshape(EPD, CAP, SUB)

    def dispatch(i, _):
        outbuf[i] = gathered(partner_to(e, i))
        sending(i).start()
        return 0

    lax.fori_loop(0, NE - 1, dispatch, 0)
    arrived[e] = gathered(e)

    logits = jnp.dot(xbuf[...].reshape(SUB, SUB), rw_ref[...], preferred_element_type=f32)
    lanes64 = lax.broadcasted_iota(jnp.int32, (SUB, 64), 1).astype(f32)
    picked = [
        jnp.sum(jnp.where(lanes64 == cols[2 + t][:, 0:64], logits, 0.0), axis=1, keepdims=True) for t in range(2)
    ]
    sig0 = 1.0 / (1.0 + jnp.exp(-picked[0]))
    sig1 = 1.0 / (1.0 + jnp.exp(-picked[1]))
    cols[2] = jnp.broadcast_to(sig0 / (sig0 + sig1), (SUB, HD))
    cols[3] = jnp.broadcast_to(sig1 / (sig0 + sig1), (SUB, HD))
    acc[...] = jnp.zeros((SUB, SUB), f32)

    for copy in loads:
        copy.wait()

    def giving(i):
        return remote(res.at[i], returned.at[e], rsend.at[i], rrecv.at[e], s, partner_from(e, i))

    def group(q, _):
        sources = [partner_from(e, q * 4 + j) for j in range(4)]
        for j in range(4):
            src = sources[j]

            @pl.when(src != e)
            def _():
                pltpu.make_async_copy(arrived.at[src], arrived.at[src], drecv.at[src]).wait()

        def one(xp, _):
            a = jnp.concatenate([arrived[src, xp] for src in sources], axis=0)
            u = jnp.dot(a, win[xp], preferred_element_type=f32)
            hid = 0.5 * u * (1.0 + jnp.tanh(0.7978845608028654 * (u + 0.044715 * (u * u * u))))
            y = jnp.dot(hid.astype(bf16), wout[xp], preferred_element_type=f32).astype(bf16)
            for j in range(4):
                res[q * 4 + j, xp] = y[j * CAP:(j + 1) * CAP]
            return 0

        lax.fori_loop(0, EPD, one, 0)
        for j in range(4):
            i = q * 4 + j

            @pl.when(i != NE - 1)
            def _():
                giving(i).start()

        return 0

    lax.fori_loop(0, 4, group, 0)
    returned[e] = res[NE - 1]

    lane = lax.broadcasted_iota(jnp.int32, (SUB, HD), 1)

    def combine(p, _):
        parts = []
        tables = []
        for j in range(2):
            d = partner_to(e, 2 * p + j)

            @pl.when(d != e)
            def _():
                pltpu.make_async_copy(returned.at[d], returned.at[d], rrecv.at[d]).wait()

            slot = (lane + d * ROWS).astype(f32)
            tables.append(
                jnp.where(slot == cols[0], cols[2], 0.0) + jnp.where(slot == cols[1], cols[3], 0.0)
            )
            parts.append(returned[d].reshape(ROWS, SUB))
        table = jnp.concatenate(tables, axis=1)
        rows = jnp.concatenate(parts, axis=0)
        high = table.astype(bf16)
        low = (table - high.astype(f32)).astype(bf16)
        acc[...] += jnp.dot(high, rows, preferred_element_type=f32) + jnp.dot(low, rows, preferred_element_type=f32)
        return 0

    lax.fori_loop(0, NE // 2, combine, 0)
    for b in range(SEQS):
        for g in range(4):
            mix_ref[b, :, g * SUB:(g + 1) * SUB] = acc[(b * 4 + g) * TOK:(b * 4 + g + 1) * TOK].astype(bf16)

    pltpu.make_async_copy(obuf, obuf, osend).wait()

    def drain(j, _):
        for copy in sends(j) + forward(j):
            copy.wait_send()
        return 0

    lax.fori_loop(1, SEQS, drain, 0)
    for copy in near:
        copy.wait_send()

    def drain_rows(i, _):
        sending(i).wait_send()
        giving(i).wait_send()
        return 0

    lax.fori_loop(0, NE - 1, drain_rows, 0)


def body(queries, keys, values, seg_ids, norm_gain, router_w, expert_ids, w_in, w_out):
    ids = expert_ids.transpose(3, 1, 2, 0).reshape(2, SUB)
    vmem = pl.BlockSpec(memory_space=pltpu.VMEM)
    hbm = pl.BlockSpec(memory_space=pl.ANY)
    dma = pltpu.SemaphoreType.DMA
    bf16, f32 = jnp.bfloat16, jnp.float32
    return pl.pallas_call(
        kernel,
        out_shape=(
            jax.ShapeDtypeStruct((SEQS, TOK, 2048), bf16),
            jax.ShapeDtypeStruct((SEQS, TOK, 2048), bf16),
        ),
        in_specs=[hbm] * 3 + [vmem] * 4 + [hbm] * 2,
        out_specs=(vmem, vmem),
        scratch_shapes=[
            pltpu.VMEM((NS, HALF, HD), bf16),
            pltpu.VMEM((NS, BLK, HD), bf16),
            pltpu.VMEM((NS, BLK, HD), bf16),
            pltpu.VMEM((GROUPS, QG, HD), bf16),
            pltpu.VMEM((GROUPS, KC, HD), bf16),
            pltpu.VMEM((2, GROUPS, QG, KC), f32),
            pltpu.VMEM((2, QG, HD), f32),
            pltpu.VMEM((QG, HD), f32),
            pltpu.VMEM((QG, HD), f32),
            pltpu.VMEM((QG, HD), f32),
            pltpu.VMEM((NS, 8, TOK, HD), bf16),
            pltpu.VMEM((SEQS, NE, TOK, HD), bf16),
            pltpu.VMEM((32, TOK, SUB), bf16),
            pltpu.VMEM((NE, EPD, CAP, SUB), bf16),
            pltpu.VMEM((NE, EPD, CAP, SUB), bf16),
            pltpu.VMEM((NE, EPD, CAP, SUB), bf16),
            pltpu.VMEM((NE, EPD, CAP, SUB), bf16),
            pltpu.VMEM((EPD, SUB, FFH), bf16),
            pltpu.VMEM((EPD, FFH, SUB), bf16),
            pltpu.VMEM((SUB, SUB), f32),
            pltpu.VMEM((4, SUB, HD), f32),
            pltpu.VMEM((TOK, HD), bf16),
            pltpu.SemaphoreType.REGULAR,
            dma((3,)), dma((SEQS,)), dma((SEQS,)), dma((2 * SEQS,)),
            dma((NS,)), dma((NS,)), dma((NS,)), dma((SEQS,)), dma((SEQS,)),
            dma((2,)), dma(()), dma((SEQS,)), dma((NE,)), dma((NE,)), dma((NE,)), dma((NE,)),
        ],
        compiler_params=pltpu.CompilerParams(
            collective_id=0, has_side_effects=True, vmem_limit_bytes=56 * 1024 * 1024
        ),
        name="block",
    )(
        queries.reshape(SEQS, 2, HALF, HD), keys, values, seg_ids, ids,
        norm_gain.reshape(16, HD), router_w, w_in, w_out,
    )


def solution(mesh):
    return jax.shard_map(
        body,
        mesh=mesh,
        in_specs=(
            P(None, "seq", "exp"),
            P(None, "seq", "exp"),
            P(None, "seq", "exp"),
            P(),
            P(),
            P(),
            P(("seq", "exp"), None, None, None),
            P("exp", None, None),
            P("exp", None, None),
        ),
        out_specs=(P(None, ("seq", "exp"), None), P(None, ("seq", "exp"), None)),
        check_vma=False,
    )
```

time: 195 us -> 172 us (0.88)
  the two profiles are of different devices: /device:TPU:120 before, /device:TPU:1 now
where the time goes in v2:
time: 172 us; the launch traced here: 171 us
  Pallas kernels  163 us (95%)
  local copies, waits for them, and re-layouts  6.81 us (4%)
    pallas_call x1, Pallas kernels, body(): pl.pallas_call(kernel, out_shape=(jax.ShapeDtypeStruct((SEQS, TOK, 2048),...  163 us
    unnamed x3, local copies, waits for them, and re-layouts  5.36 us

profile of v2, /device:TPU:1, one launch (start us, length us, event | category | flops | bytes accessed | tf_op | source)
XLA Modules:
  0.0 170.7 jit_solution(13544155108837126363)
XLA Ops:
  0.6 0.8 copy.11
  1.4 0.7 reshape.14.ids_ref
  2.1 1.6 copy.12.rw_ref
  3.7 163.3 %block.1 = (bf16[8,16,2048]{2,1,0:T(8,128)(2,1)}, bf16[8,16,2048]{2,1,0:T(8,128)(2,1)}) custom-call(bf16[8,2,128,128]{3,2,1,0:T(8,128)(2,1)} %bitcast.3, bf16[8,256,128]{2,1,0:T(8,128)(2,1)} %k_ref.1, bf16[8,256,128]{2,1,0:T(8,128)(2,1)} %v_ref.1, s32[8,4096]{1,0:T(8,128)} %seg_ref.1, s32[2,512]{1,0:T(2,128)} %reshape.14.ids_ref, f32[16,128]{1,0:T(8,128)} %bitcast.5, ...), custom_call_target="tpu_custom_call" | custom-call | tf_op jit(solution)/shard_map/block/pallas_call | solution.py:432
  167.0 1.9 %copy.15 = bf16[8,16,2048]{2,1,0:T(8,128)(2,1)} copy(bf16[8,16,2048]{2,1,0:T(8,128)(2,1)} %get-tuple-element.4) | data formatting | bytes 1048576
  168.9 1.9 %copy.16 = bf16[8,16,2048]{2,1,0:T(8,128)(2,1)} copy(bf16[8,16,2048]{2,1,0:T(8,128)(2,1)} %get-tuple-element.5) | data formatting | bytes 1048576

commit v3 on v2

--- a/solution.py
+++ b/solution.py
@@ -87,23 +87,27 @@
             src_ref=src, dst_ref=dst, send_sem=ss, recv_sem=rs, device_id=other(seq, exp), device_id_type=MESH
         )
 
-    def sends(j):
+    def send(which, j):
         b = (c + j) % SEQS
         same = 2 * b + k
         cross = 2 * b + 1 - k
-        return (
-            remote(k_ref.at[b], kbuf.at[s], ksend.at[j], krecv.at[s], same, e),
-            remote(v_ref.at[b], vbuf.at[s], vsend.at[j], vrecv.at[s], same, e),
-            remote(q_ref.at[b, k], qbuf.at[s], qsend.at[j], qrecv.at[s], same, e),
-            remote(q_ref.at[b, 1 - k], qbuf.at[s], qsend.at[SEQS + j], qrecv.at[s], cross, e),
-        )
-
-    def start(j, _):
-        for copy in sends(j):
-            copy.start()
-        return 0
-
-    lax.fori_loop(1, SEQS, start, 0)
+        if which == 0:
+            return remote(k_ref.at[b], kbuf.at[s], ksend.at[j], krecv.at[s], same, e)
+        if which == 1:
+            return remote(q_ref.at[b, k], qbuf.at[s], qsend.at[j], qrecv.at[s], same, e)
+        if which == 2:
+            return remote(q_ref.at[b, 1 - k], qbuf.at[s], qsend.at[SEQS + j], qrecv.at[s], cross, e)
+        return remote(v_ref.at[b], vbuf.at[s], vsend.at[j], vrecv.at[s], same, e)
+
+    def start_with(*which):
+        def start(j, _):
+            for i in which:
+                send(i, j).start()
+            return 0
+
+        lax.fori_loop(1, SEQS, start, 0)
+
+    start_with(0)
     own = (
         pltpu.make_async_copy(k_ref.at[c], kbuf.at[s], loc.at[0]),
         pltpu.make_async_copy(v_ref.at[c], vbuf.at[s], loc.at[1]),
@@ -114,7 +118,11 @@
         remote(v_ref.at[c], vbuf.at[s], vfwd.at[0], vrecv.at[s], other_core, e),
         remote(q_ref.at[c, 1 - k], qbuf.at[s], qsend.at[0], qrecv.at[s], other_core, e),
     )
-    for copy in own + near + loads:
+    for copy in own + near:
+        copy.start()
+    start_with(3)
+    start_with(1, 2)
+    for copy in loads:
         copy.start()
 
     def greet_again(i, _):
@@ -141,53 +149,57 @@
 
     lax.fori_loop(0, GROUPS, mark, 0)
 
-    ids = ids_ref[...]
-    experts = lax.broadcasted_iota(jnp.int32, (64, SUB), 0)
+    to_lane = (
+        lax.broadcasted_iota(jnp.int32, (TOK, SUB), 0) == lax.broadcasted_iota(jnp.int32, (TOK, SUB), 1) % TOK
+    ).astype(f32).astype(bf16)
+    own_row = lax.broadcasted_iota(jnp.int32, (32, SUB), 0) == lax.broadcasted_iota(jnp.int32, (32, SUB), 1) // TOK
+    ids = []
+    for t in range(2):
+        table = jnp.dot(ids_ref[:, t, :].astype(f32).astype(bf16), to_lane, preferred_element_type=f32)
+        ids.append(jnp.sum(jnp.where(own_row, table, 0.0), axis=0, keepdims=True))
+    experts = lax.broadcasted_iota(jnp.int32, (64, SUB), 0).astype(f32)
     before = (
         lax.broadcasted_iota(jnp.int32, (SUB, SUB), 0) < lax.broadcasted_iota(jnp.int32, (SUB, SUB), 1)
     ).astype(f32).astype(bf16)
-    hot0 = (experts == ids[0:1]).astype(f32)
-    hot1 = (experts == ids[1:2]).astype(f32)
+    hot0 = (experts == ids[0]).astype(f32)
+    hot1 = (experts == ids[1]).astype(f32)
     run0 = jnp.dot(hot0.astype(bf16), before, preferred_element_type=f32)
     run1 = jnp.dot(hot1.astype(bf16), before, preferred_element_type=f32)
     run1 = run1 + jnp.sum(hot0, axis=1, keepdims=True)
-    idf = ids.astype(f32)
-    slot0 = idf[0:1] * CAP + jnp.sum(run0 * hot0, axis=0, keepdims=True)
-    slot1 = idf[1:2] * CAP + jnp.sum(run1 * hot1, axis=0, keepdims=True)
-    lines = jnp.concatenate([slot0, slot1, idf, jnp.zeros((124, SUB), f32)], axis=0)
+    slot0 = ids[0] * CAP + jnp.sum(run0 * hot0, axis=0, keepdims=True)
+    slot1 = ids[1] * CAP + jnp.sum(run1 * hot1, axis=0, keepdims=True)
+    lines = jnp.concatenate([slot0, slot1, *ids, jnp.zeros((124, SUB), f32)], axis=0)
     lines = jnp.transpose(lines)
     for i in range(4):
         cols[i] = jnp.broadcast_to(lines[:, i:i + 1], (SUB, HD))
 
-    def forward(j):
+    def forward(which, j):
         src = 2 * ((c + SEQS - j) % SEQS) + k
-        return (
-            remote(kbuf.at[src], kbuf.at[src], kfwd.at[j], krecv.at[src], other_core, e),
-            remote(vbuf.at[src], vbuf.at[src], vfwd.at[j], vrecv.at[src], other_core, e),
-        )
-
-    def relay(j, _):
-        for copy in forward(j):
+        if which == 0:
+            return remote(kbuf.at[src], kbuf.at[src], kfwd.at[j], krecv.at[src], other_core, e)
+        return remote(vbuf.at[src], vbuf.at[src], vfwd.at[j], vrecv.at[src], other_core, e)
+
+    def relay_of(which):
+        def relay(j, _):
+            copy = forward(which, j)
             copy.wait_recv()
             copy.start()
-        return 0
-
-    lax.fori_loop(1, SEQS, relay, 0)
-
-    def finish(j, _):
-        src = 2 * ((c + SEQS - j) % SEQS) + 1 - k
-        pltpu.make_async_copy(kbuf.at[src], kbuf.at[src], krecv.at[src]).wait()
-        pltpu.make_async_copy(vbuf.at[src], vbuf.at[src], vrecv.at[src]).wait()
-        return 0
-
-    lax.fori_loop(0, SEQS, finish, 0)
-
-    def finish_q(i, _):
-        src = (s + i) % NS
-        pltpu.make_async_copy(qbuf.at[src], qbuf.at[src], qrecv.at[src]).wait()
-        return 0
-
-    lax.fori_loop(1, NS, finish_q, 0)
+            return 0
+
+        lax.fori_loop(1, SEQS, relay, 0)
+
+    def finish_of(buf, sem):
+        def finish(j, _):
+            src = 2 * ((c + SEQS - j) % SEQS) + 1 - k
+            pltpu.make_async_copy(buf.at[src], buf.at[src], sem.at[src]).wait()
+            return 0
+
+        lax.fori_loop(0, SEQS, finish, 0)
+
+    relay_of(0)
+    relay_of(1)
+    finish_of(kbuf, krecv)
+    finish_of(vbuf, vrecv)
     for copy in own:
         copy.wait()
     pl.semaphore_wait(ready, NE - 1)
@@ -205,89 +217,84 @@
             out = op(out, x[:, i * HD:(i + 1) * HD])
         return out
 
-    def first_pass(m, j):
-        scores = scores_of(m, j)
-        sbuf[m % 2, j] = scores
-        pmax[m % 2] = jnp.maximum(pmax[m % 2], tiles(scores, jnp.maximum))
-
-    def diagonal(m):
+    def first_pass(m, j, count):
+        highest = pmax[...]
+        for i in range(count):
+            scores = scores_of(m, j + i)
+            sbuf[j + i] = scores
+            highest = jnp.maximum(highest, tiles(scores, jnp.maximum))
+        pmax[...] = highest
+
+    def second_pass(m, j, count):
+        top = jnp.concatenate([mrow[...]] * (KC // HD), axis=1)
+        total = asum[...]
+        out = aacc[...]
+        for i in range(count):
+            weights = jnp.exp2((sbuf[j + i] - top) * scale)
+            total = total + tiles(weights, jnp.add)
+            vv = vbuf[pl.ds(2 * (j + i), 2)].reshape(KC, HD)
+            out = out + jnp.dot(weights.astype(bf16), vv, preferred_element_type=f32)
+        asum[...] = total
+        aacc[...] = out
+
+    def attend(t, _):
+        m = (c + GROUPS - t) % GROUPS
+        for i in range(2):
+            src = 2 * m + i
+
+            @pl.when(src != s)
+            def _():
+                pltpu.make_async_copy(qbuf.at[src], qbuf.at[src], qrecv.at[src]).wait()
+
+        pmax[...] = jnp.full((QG, HD), -BIG, f32)
+        asum[...] = jnp.zeros((QG, HD), f32)
+        aacc[...] = jnp.zeros((QG, HD), f32)
+
+        def score(j, _):
+            first_pass(m, 2 * j, 2)
+            return 0
+
+        lax.fori_loop(0, m // 2, score, 0)
+
+        @pl.when(m % 2 == 1)
+        def _():
+            first_pass(m, m - 1, 1)
+
         scores = scores_of(m, m)
         row = lax.broadcasted_iota(jnp.int32, (QG, KC), 0)
         row = row + jnp.where(row >= HALF, HALF, 0) + k * HALF
         scores = jnp.where(lax.broadcasted_iota(jnp.int32, (QG, KC), 1) <= row, scores, -BIG)
-        sbuf[m % 2, m] = scores
-        highest = jnp.maximum(pmax[m % 2], tiles(scores, jnp.maximum))
+        sbuf[m] = scores
+        highest = jnp.maximum(pmax[...], tiles(scores, jnp.maximum))
         mrow[...] = jnp.broadcast_to(jnp.max(highest, axis=-1, keepdims=True), (QG, HD))
 
-    def second_pass(m, j):
-        top = mrow[...]
-        top = jnp.concatenate([top] * (KC // HD), axis=1)
-        weights = jnp.exp2((sbuf[m % 2, j] - top) * scale)
-        asum[...] += tiles(weights, jnp.add)
-        vv = vbuf[pl.ds(2 * j, 2)].reshape(KC, HD)
-        aacc[...] += jnp.dot(weights.astype(bf16), vv, preferred_element_type=f32)
-
-    def clear(m):
-        pmax[m % 2] = jnp.full((QG, HD), -BIG, f32)
-
-    def only_first(j, _):
-        first_pass(c, j)
-        return 0
-
-    clear(c)
-    lax.fori_loop(0, c, only_first, 0)
-    diagonal(c)
-
-    def attend(t, _):
-        m = (c + t) % GROUPS
-        after = (m + 1) % GROUPS
-        asum[...] = jnp.zeros((QG, HD), f32)
-        aacc[...] = jnp.zeros((QG, HD), f32)
-        clear(after)
-        both = (m < GROUPS - 1) & (t < GROUPS - 1)
-
-        @pl.when(both)
+        def step(j, _):
+            second_pass(m, 2 * j, 2)
+            return 0
+
+        lax.fori_loop(0, (m + 1) // 2, step, 0)
+
+        @pl.when(m % 2 == 0)
         def _():
-            def step(j, _):
-                first_pass(m + 1, j)
-                second_pass(m, j)
-                return 0
-
-            lax.fori_loop(0, m + 1, step, 0)
-
-        @pl.when(jnp.logical_not(both))
-        def _():
-            def step(j, _):
-                second_pass(m, j)
-                return 0
-
-            lax.fori_loop(0, m + 1, step, 0)
+            second_pass(m, m, 1)
 
         total = jnp.sum(asum[...], axis=-1, keepdims=True)
         obuf[pl.ds(2 * m, 2)] = (aacc[...] / total).astype(bf16).reshape(2, 8, TOK, HD)
 
-        def give(i, _):
+        for i in range(16):
             sp = 2 * m + i // 8
             ei = (e + i) % 8
-            ep = k * 8 + ei
-            mine = (sp == s) & (ep == e)
-
-            @pl.when(jnp.logical_not(mine))
-            def _():
-                remote(obuf.at[sp, ei], tok.at[c, e], osend, orecv.at[c], sp, ep).start()
+            copy = remote(obuf.at[sp, ei], tok.at[c, e], osend, orecv.at[c], sp, k * 8 + ei)
+            if i % 8:
+                copy.start()
+                continue
+            mine = (sp == s) & (k == e // 8)
+            pl.when(jnp.logical_not(mine))(copy.start)
 
             @pl.when(mine)
             def _():
                 pltpu.make_async_copy(obuf.at[sp, ei], tok.at[c, e], orecv.at[c]).start()
                 pltpu.make_async_copy(obuf.at[sp, ei], spare, osend).start()
-
-            return 0
-
-        lax.fori_loop(0, 16, give, 0)
-
-        @pl.when(t < GROUPS - 1)
-        def _():
-            diagonal(after)
 
         return 0
 
@@ -327,7 +334,9 @@
     lax.fori_loop(0, NE - 1, dispatch, 0)
     arrived[e] = gathered(e)
 
-    logits = jnp.dot(xbuf[...].reshape(SUB, SUB), rw_ref[...], preferred_element_type=f32)
+    logits = lax.dot_general(
+        xbuf[...].reshape(SUB, SUB), rw_ref[...], (((1,), (1,)), ((), ())), preferred_element_type=f32
+    )
     lanes64 = lax.broadcasted_iota(jnp.int32, (SUB, 64), 1).astype(f32)
     picked = [
         jnp.sum(jnp.where(lanes64 == cols[2 + t][:, 0:64], logits, 0.0), axis=1, keepdims=True) for t in range(2)
@@ -407,8 +416,10 @@
     pltpu.make_async_copy(obuf, obuf, osend).wait()
 
     def drain(j, _):
-        for copy in sends(j) + forward(j):
-            copy.wait_send()
+        for i in range(4):
+            send(i, j).wait_send()
+        for i in range(2):
+            forward(i, j).wait_send()
         return 0
 
     lax.fori_loop(1, SEQS, drain, 0)
@@ -424,7 +435,7 @@
 
 
 def body(queries, keys, values, seg_ids, norm_gain, router_w, expert_ids, w_in, w_out):
-    ids = expert_ids.transpose(3, 1, 2, 0).reshape(2, SUB)
+    ids = expert_ids.transpose(1, 2, 3, 0).reshape(32, 2, TOK)
     vmem = pl.BlockSpec(memory_space=pltpu.VMEM)
     hbm = pl.BlockSpec(memory_space=pl.ANY)
     dma = pltpu.SemaphoreType.DMA
@@ -443,8 +454,8 @@
             pltpu.VMEM((NS, BLK, HD), bf16),
             pltpu.VMEM((GROUPS, QG, HD), bf16),
             pltpu.VMEM((GROUPS, KC, HD), bf16),
-            pltpu.VMEM((2, GROUPS, QG, KC), f32),
-            pltpu.VMEM((2, QG, HD), f32),
+            pltpu.VMEM((GROUPS, QG, KC), f32),
+            pltpu.VMEM((QG, HD), f32),
             pltpu.VMEM((QG, HD), f32),
             pltpu.VMEM((QG, HD), f32),
             pltpu.VMEM((QG, HD), f32),
@@ -471,7 +482,7 @@
         name="block",
     )(
         queries.reshape(SEQS, 2, HALF, HD), keys, values, seg_ids, ids,
-        norm_gain.reshape(16, HD), router_w, w_in, w_out,
+        norm_gain.reshape(16, HD), router_w.T, w_in, w_out,
     )
 
 

time: 172 us -> 155 us (0.901)
  Pallas kernels: 163 us -> 150 us
  local copies, waits for them, and re-layouts: 6.81 us -> 3.76 us
    pallas_call x1, Pallas kernels: 163 us -> 150 us  [body(): pl.pallas_call(kernel, out_shape=(jax.ShapeDtypeStruct((SEQS, TOK, 2048),...]
    unnamed x3 -> x2, local copies, waits for them, and re-layouts: 5.36 us -> 3.76 us
where the time goes in v3:
time: 155 us; the launch traced here: 154 us
  Pallas kernels  150 us (97%)
  local copies, waits for them, and re-layouts  3.76 us (2%)
    pallas_call x1, Pallas kernels, body(): pl.pallas_call(kernel, out_shape=(jax.ShapeDtypeStruct((SEQS, TOK, 2048),...  150 us
    unnamed x2, local copies, waits for them, and re-layouts  3.76 us

profile of v3, /device:TPU:1, one launch (start us, length us, event | category | flops | bytes accessed | tf_op | source)
XLA Modules:
  0.0 154.4 jit_solution(11738641199727769911)
XLA Ops:
  0.6 150.0 %block.1 = (bf16[8,16,2048]{2,1,0:T(8,128)(2,1)}, bf16[8,16,2048]{2,1,0:T(8,128)(2,1)}) custom-call(bf16[8,2,128,128]{3,2,1,0:T(8,128)(2,1)} %bitcast.6, bf16[8,256,128]{2,1,0:T(8,128)(2,1)} %k_ref.1, bf16[8,256,128]{2,1,0:T(8,128)(2,1)} %v_ref.1, s32[8,4096]{1,0:T(8,128)} %seg_ref.1, s32[32,2,16]{2,1,0:T(2,128)} %bitcast.8, f32[16,128]{1,0:T(8,128)} %bitcast.9, ...), custom_call_target="tpu_custom_call" | custom-call | tf_op jit(solution)/shard_map/block/pallas_call | solution.py:443
  150.6 1.9 %copy.13 = bf16[8,16,2048]{2,1,0:T(8,128)(2,1)} copy(bf16[8,16,2048]{2,1,0:T(8,128)(2,1)} %get-tuple-element.4) | data formatting | bytes 1048576
  152.5 1.9 %copy.14 = bf16[8,16,2048]{2,1,0:T(8,128)(2,1)} copy(bf16[8,16,2048]{2,1,0:T(8,128)(2,1)} %get-tuple-element.5) | data formatting | bytes 1048576

commit v4 on v3

--- a/solution.py
+++ b/solution.py
@@ -53,12 +53,38 @@
     return (e // NZ + dy) % 2 * NZ + (e % NZ + NZ - dz) % NZ
 
 
+def region(i):
+    if isinstance(i, int) and i < 2:
+        return 2 * i, 2
+    if isinstance(i, int) and i == NE:
+        return 60, 2
+    return EPD * (i - 1), EPD
+
+
+def experts_of(e, chunk):
+    def of(i):
+        d = partner_to(e, i)
+        y, z = d // NZ, d % NZ
+        return EPD * d, EPD * (y * NZ + (z + NZ - 1) % NZ), EPD * (y * NZ + (z + 1) % NZ)
+
+    if isinstance(chunk, int) and chunk == 0:
+        first, second = of(0)[0], of(1)[0]
+        return first + 2, first + 3, second + 2, second + 3
+    if isinstance(chunk, int) and chunk == NE - 1:
+        (first, before, _), (second, before2, _) = of(NE - 2), of(NE - 1)
+        return first + 1, before, second + 1, before2
+    i = chunk + 1
+    home, before, after = of(i)
+    up = (i // 2) % 2 == 1
+    return home + 2, home + 3, jnp.where(up, home, home + 1), jnp.where(up, after + 1, before)
+
+
 def kernel(
     q_ref, k_ref, v_ref, seg_ref, ids_ref, gain_ref, rw_ref, win_hbm, wout_hbm, normed_ref, mix_ref,
     qbuf, kbuf, vbuf, qaug, kaug, sbuf, pmax, mrow, asum, aacc, obuf,
     tok, xbuf, outbuf, arrived, res, returned, win, wout, acc, cols, spare,
     ready, loc, ksend, vsend, qsend, krecv, vrecv, qrecv, kfwd, vfwd,
-    wsem, osend, orecv, dsend, drecv, rsend, rrecv,
+    wsem, osend, orecv, dsend, drecv, rsend, rrecv, wsend, wrecv, wsend2,
 ):
     s = lax.axis_index("seq")
     e = lax.axis_index("exp")
@@ -68,8 +94,8 @@
     f32, bf16 = jnp.float32, jnp.bfloat16
 
     loads = (
-        pltpu.make_async_copy(win_hbm, win, wsem.at[0]),
-        pltpu.make_async_copy(wout_hbm, wout, wsem.at[1]),
+        pltpu.make_async_copy(win_hbm, win.at[pl.ds(0, EPD)], wsem.at[0]),
+        pltpu.make_async_copy(wout_hbm, wout.at[pl.ds(0, EPD)], wsem.at[1]),
     )
 
     barrier = pltpu.get_barrier_semaphore()
@@ -106,6 +132,22 @@
             return 0
 
         lax.fori_loop(1, SEQS, start, 0)
+
+    def copy_weights(part, j):
+        src, dst = (win_hbm, win) if part == 0 else (wout_hbm, wout)
+        z = (e % NZ + (1 if j == 0 else NZ - 1)) % NZ
+        return remote(src.at[j], dst.at[EPD + j], wsend.at[j], wrecv.at[part, j], s, e // NZ * NZ + z)
+
+    def pass_weights(part, j):
+        buf = win if part == 0 else wout
+        return remote(buf.at[EPD + j], buf.at[EPD + j], wsend2.at[j], wrecv.at[part, j], other_core, e)
+
+    for part in range(2):
+
+        @pl.when(k == part)
+        def _():
+            copy_weights(part, 0).start()
+            copy_weights(part, 1).start()
 
     start_with(0)
     own = (
@@ -300,6 +342,15 @@
 
     lax.fori_loop(0, GROUPS, attend, 0)
 
+    for part in range(2):
+
+        @pl.when(k == part)
+        def _():
+            for j in range(2):
+                copy = pass_weights(part, j)
+                copy.wait_recv()
+                copy.start()
+
     gain = gain_ref[...]
 
     def norm(b, _):
@@ -315,24 +366,38 @@
 
     lax.fori_loop(0, SEQS, norm, 0)
 
+    def rows_at(buf, i):
+        first, count = region(i)
+        return buf.at[pl.ds(first, count)]
+
     def sending(i):
-        return remote(outbuf.at[i], arrived.at[e], dsend.at[i], drecv.at[e], s, partner_to(e, i))
-
-    slot_line = lax.broadcasted_iota(jnp.int32, (ROWS, SUB), 0)
-
-    def gathered(d):
-        slot = (slot_line + d * ROWS).astype(f32)
+        return remote(
+            rows_at(outbuf, i), rows_at(arrived, i), dsend.at[i], drecv.at[i], s, partner_to(e, 14 if isinstance(i, int) and i == NE else i)
+        )
+
+    slot_line = lax.broadcasted_iota(jnp.int32, (CAP, SUB), 0)
+
+    def gathered(chunk):
+        slot = jnp.concatenate([slot_line + x * CAP for x in experts_of(e, chunk)], axis=0).astype(f32)
         chosen = ((slot == slot0) | (slot == slot1)).astype(f32).astype(bf16)
         rows = jnp.dot(chosen, xbuf[...].reshape(SUB, SUB), preferred_element_type=f32)
         return rows.astype(bf16).reshape(EPD, CAP, SUB)
 
+    outbuf[0:EPD] = gathered(0)
+    sending(0).start()
+    sending(1).start()
+
     def dispatch(i, _):
-        outbuf[i] = gathered(partner_to(e, i))
+        outbuf[pl.ds(EPD * (i - 1), EPD)] = gathered(i - 1)
         sending(i).start()
         return 0
 
-    lax.fori_loop(0, NE - 1, dispatch, 0)
-    arrived[e] = gathered(e)
+    lax.fori_loop(2, NE - 1, dispatch, 0)
+    rest = gathered(NE - 1)
+    outbuf[60:62] = rest[0:2]
+    sending(NE).start()
+    arrived[62:64] = rest[2:4]
+    arrived[56:60] = gathered(NE - 2)
 
     logits = lax.dot_general(
         xbuf[...].reshape(SUB, SUB), rw_ref[...], (((1,), (1,)), ((), ())), preferred_element_type=f32
@@ -349,66 +414,88 @@
 
     for copy in loads:
         copy.wait()
+    for part in range(2):
+
+        @pl.when(k != part)
+        def _():
+            for j in range(2):
+                buf = (win if part == 0 else wout).at[EPD + j]
+                pltpu.make_async_copy(buf, buf, wrecv.at[part, j]).wait()
 
     def giving(i):
-        return remote(res.at[i], returned.at[e], rsend.at[i], rrecv.at[e], s, partner_from(e, i))
-
-    def group(q, _):
-        sources = [partner_from(e, q * 4 + j) for j in range(4)]
-        for j in range(4):
-            src = sources[j]
-
-            @pl.when(src != e)
-            def _():
-                pltpu.make_async_copy(arrived.at[src], arrived.at[src], drecv.at[src]).wait()
-
+        return remote(
+            rows_at(res, i), rows_at(returned, i), rsend.at[i], rrecv.at[i], s, partner_from(e, 14 if isinstance(i, int) and i == NE else i)
+        )
+
+    def run_experts(blocks, first, step):
         def one(xp, _):
-            a = jnp.concatenate([arrived[src, xp] for src in sources], axis=0)
-            u = jnp.dot(a, win[xp], preferred_element_type=f32)
+            w = first + step * xp
+            a = jnp.concatenate([arrived[at + xp] for at in blocks], axis=0)
+            u = jnp.dot(a, win[w], preferred_element_type=f32)
             hid = 0.5 * u * (1.0 + jnp.tanh(0.7978845608028654 * (u + 0.044715 * (u * u * u))))
-            y = jnp.dot(hid.astype(bf16), wout[xp], preferred_element_type=f32).astype(bf16)
+            y = jnp.dot(hid.astype(bf16), wout[w], preferred_element_type=f32).astype(bf16)
             for j in range(4):
-                res[q * 4 + j, xp] = y[j * CAP:(j + 1) * CAP]
+                res[blocks[j] + xp] = y[j * CAP:(j + 1) * CAP]
             return 0
 
-        lax.fori_loop(0, EPD, one, 0)
-        for j in range(4):
-            i = q * 4 + j
-
-            @pl.when(i != NE - 1)
-            def _():
-                giving(i).start()
-
-        return 0
-
-    lax.fori_loop(0, 4, group, 0)
-    returned[e] = res[NE - 1]
+        lax.fori_loop(0, 2, one, 0)
+
+    plan = (
+        ((0, 1, 2, 3, 6, 7), (0, 2, 4, 8), (6, 10, 22, 26), (0, 1, 2, 3)),
+        ((4, 5, 8, 9), (12, 16, 20, 24), (14, 18, 30, 34), (4, 5, 6, 7)),
+        ((10, 11, 14), (28, 32, 36, 40), (38, 42, 54, 58), (8, 9, 10, 11)),
+        ((12, 13, 16), (44, 48, 52, 56), (46, 50, 60, 62), (12, 13, 14, 16)),
+    )
+    for q, (needed, always, shared, done) in enumerate(plan):
+        for i in needed:
+            part = rows_at(arrived, i)
+            pltpu.make_async_copy(part, part, drecv.at[i]).wait()
+        run_experts(always, 2, 1)
+        if q % 2 == 0:
+            run_experts(shared, 0, 5)
+        else:
+            run_experts(shared, 1, 3)
+        for i in done:
+            giving(i).start()
+    returned[56:60] = res[56:60]
+    returned[62:64] = res[62:64]
 
     lane = lax.broadcasted_iota(jnp.int32, (SUB, HD), 1)
 
-    def combine(p, _):
-        parts = []
-        tables = []
-        for j in range(2):
-            d = partner_to(e, 2 * p + j)
-
-            @pl.when(d != e)
-            def _():
-                pltpu.make_async_copy(returned.at[d], returned.at[d], rrecv.at[d]).wait()
-
-            slot = (lane + d * ROWS).astype(f32)
-            tables.append(
-                jnp.where(slot == cols[0], cols[2], 0.0) + jnp.where(slot == cols[1], cols[3], 0.0)
-            )
-            parts.append(returned[d].reshape(ROWS, SUB))
+    def table_of(chunk):
+        x = experts_of(e, chunk)
+        part = lane // CAP
+        slot = jnp.where(part < 2, jnp.where(part == 0, x[0], x[1]), jnp.where(part == 2, x[2], x[3]))
+        slot = (slot * CAP + lane % CAP).astype(f32)
+        return jnp.where(slot == cols[0], cols[2], 0.0) + jnp.where(slot == cols[1], cols[3], 0.0)
+
+    def add_rows(tables, parts):
         table = jnp.concatenate(tables, axis=1)
         rows = jnp.concatenate(parts, axis=0)
         high = table.astype(bf16)
         low = (table - high.astype(f32)).astype(bf16)
         acc[...] += jnp.dot(high, rows, preferred_element_type=f32) + jnp.dot(low, rows, preferred_element_type=f32)
-        return 0
-
-    lax.fori_loop(0, NE // 2, combine, 0)
+
+    def chunk_rows(chunk):
+        return returned[pl.ds(EPD * chunk, EPD)].reshape(ROWS, SUB)
+
+    def wait_rows(i):
+        part = rows_at(returned, i)
+        pltpu.make_async_copy(part, part, rrecv.at[i]).wait()
+
+    for i in (0, 1, 2):
+        wait_rows(i)
+    add_rows([table_of(0), table_of(1)], [chunk_rows(0), chunk_rows(1)])
+
+    def combine(p, _):
+        wait_rows(2 * p + 1)
+        wait_rows(2 * p + 2)
+        add_rows([table_of(2 * p), table_of(2 * p + 1)], [chunk_rows(2 * p), chunk_rows(2 * p + 1)])
+        return 0
+
+    lax.fori_loop(1, NE // 2 - 1, combine, 0)
+    wait_rows(NE)
+    add_rows([table_of(NE - 2), table_of(NE - 1)], [chunk_rows(NE - 2), chunk_rows(NE - 1)])
     for b in range(SEQS):
         for g in range(4):
             mix_ref[b, :, g * SUB:(g + 1) * SUB] = acc[(b * 4 + g) * TOK:(b * 4 + g + 1) * TOK].astype(bf16)
@@ -431,7 +518,16 @@
         giving(i).wait_send()
         return 0
 
-    lax.fori_loop(0, NE - 1, drain_rows, 0)
+    for i in (0, 1, NE):
+        drain_rows(i, 0)
+    lax.fori_loop(2, NE - 1, drain_rows, 0)
+    for part in range(2):
+
+        @pl.when(k == part)
+        def _():
+            for j in range(2):
+                copy_weights(part, j).wait_send()
+                pass_weights(part, j).wait_send()
 
 
 def body(queries, keys, values, seg_ids, norm_gain, router_w, expert_ids, w_in, w_out):
@@ -462,19 +558,20 @@
             pltpu.VMEM((NS, 8, TOK, HD), bf16),
             pltpu.VMEM((SEQS, NE, TOK, HD), bf16),
             pltpu.VMEM((32, TOK, SUB), bf16),
-            pltpu.VMEM((NE, EPD, CAP, SUB), bf16),
-            pltpu.VMEM((NE, EPD, CAP, SUB), bf16),
-            pltpu.VMEM((NE, EPD, CAP, SUB), bf16),
-            pltpu.VMEM((NE, EPD, CAP, SUB), bf16),
-            pltpu.VMEM((EPD, SUB, FFH), bf16),
-            pltpu.VMEM((EPD, FFH, SUB), bf16),
+            pltpu.VMEM((NE * EPD, CAP, SUB), bf16),
+            pltpu.VMEM((NE * EPD, CAP, SUB), bf16),
+            pltpu.VMEM((NE * EPD, CAP, SUB), bf16),
+            pltpu.VMEM((NE * EPD, CAP, SUB), bf16),
+            pltpu.VMEM((EPD + 2, SUB, FFH), bf16),
+            pltpu.VMEM((EPD + 2, FFH, SUB), bf16),
             pltpu.VMEM((SUB, SUB), f32),
             pltpu.VMEM((4, SUB, HD), f32),
             pltpu.VMEM((TOK, HD), bf16),
             pltpu.SemaphoreType.REGULAR,
             dma((3,)), dma((SEQS,)), dma((SEQS,)), dma((2 * SEQS,)),
             dma((NS,)), dma((NS,)), dma((NS,)), dma((SEQS,)), dma((SEQS,)),
-            dma((2,)), dma(()), dma((SEQS,)), dma((NE,)), dma((NE,)), dma((NE,)), dma((NE,)),
+            dma((2,)), dma(()), dma((SEQS,)), dma((NE + 1,)), dma((NE + 1,)), dma((NE + 1,)), dma((NE + 1,)),
+            dma((2,)), dma((2, 2)), dma((2,)),
         ],
         compiler_params=pltpu.CompilerParams(
             collective_id=0, has_side_effects=True, vmem_limit_bytes=56 * 1024 * 1024

time: 155 us -> 144 us (0.929)
  Pallas kernels: 150 us -> 139 us
    pallas_call x1, Pallas kernels: 150 us -> 139 us  [body(): pl.pallas_call(kernel, out_shape=(jax.ShapeDtypeStruct((SEQS, TOK, 2048),...]
where the time goes in v4:
time: 144 us; the launch traced here: 143 us
  Pallas kernels  139 us (97%)
  local copies, waits for them, and re-layouts  3.76 us (3%)
    pallas_call x1, Pallas kernels, body(): pl.pallas_call(kernel, out_shape=(jax.ShapeDtypeStruct((SEQS, TOK, 2048),...  139 us
    unnamed x2, local copies, waits for them, and re-layouts  3.76 us

profile of v4, /device:TPU:1, one launch (start us, length us, event | category | flops | bytes accessed | tf_op | source)
XLA Modules:
  0.0 143.3 jit_solution(4368388531343220603)
XLA Ops:
  0.6 138.9 %block.1 = (bf16[8,16,2048]{2,1,0:T(8,128)(2,1)}, bf16[8,16,2048]{2,1,0:T(8,128)(2,1)}) custom-call(bf16[8,2,128,128]{3,2,1,0:T(8,128)(2,1)} %bitcast.6, bf16[8,256,128]{2,1,0:T(8,128)(2,1)} %k_ref.1, bf16[8,256,128]{2,1,0:T(8,128)(2,1)} %v_ref.1, s32[8,4096]{1,0:T(8,128)} %seg_ref.1, s32[32,2,16]{2,1,0:T(2,128)} %bitcast.8, f32[16,128]{1,0:T(8,128)} %bitcast.9, ...), custom_call_target="tpu_custom_call" | custom-call | tf_op jit(solution)/shard_map/block/pallas_call | solution.py:539
  139.6 1.9 %copy.13 = bf16[8,16,2048]{2,1,0:T(8,128)(2,1)} copy(bf16[8,16,2048]{2,1,0:T(8,128)(2,1)} %get-tuple-element.4) | data formatting | bytes 1048576
  141.5 1.9 %copy.14 = bf16[8,16,2048]{2,1,0:T(8,128)(2,1)} copy(bf16[8,16,2048]{2,1,0:T(8,128)(2,1)} %get-tuple-element.5) | data formatting | bytes 1048576

commit v5 on v4

--- a/solution.py
+++ b/solution.py
@@ -36,10 +36,11 @@
 
 def offset_of(i):
     p = i // 2
-    mag = 4 - (p + 1) // 2
-    return (i + 1) % 2, jnp.where(p % 2 == 0, NZ - mag, mag)
-
-
+    mag = 3 - p // 2
+    return (i + 1) % 2, jnp.where(p % 2 == 0, mag, NZ - mag)
+
+
+NEAR = 12
 NZ = 8
 
 
@@ -54,29 +55,20 @@
 
 
 def region(i):
-    if isinstance(i, int) and i < 2:
-        return 2 * i, 2
-    if isinstance(i, int) and i == NE:
-        return 60, 2
-    return EPD * (i - 1), EPD
+    return EPD * i, (2 * EPD if isinstance(i, int) and i == NEAR else EPD)
 
 
 def experts_of(e, chunk):
-    def of(i):
-        d = partner_to(e, i)
-        y, z = d // NZ, d % NZ
-        return EPD * d, EPD * (y * NZ + (z + NZ - 1) % NZ), EPD * (y * NZ + (z + 1) % NZ)
-
-    if isinstance(chunk, int) and chunk == 0:
-        first, second = of(0)[0], of(1)[0]
-        return first + 2, first + 3, second + 2, second + 3
-    if isinstance(chunk, int) and chunk == NE - 1:
-        (first, before, _), (second, before2, _) = of(NE - 2), of(NE - 1)
-        return first + 1, before, second + 1, before2
-    i = chunk + 1
-    home, before, after = of(i)
-    up = (i // 2) % 2 == 1
-    return home + 2, home + 3, jnp.where(up, home, home + 1), jnp.where(up, after + 1, before)
+    i = chunk if not isinstance(chunk, int) or chunk < NEAR else NEAR + (chunk - NEAR) // 2
+    d = partner_to(e, i)
+    y, z = d // NZ, d % NZ
+    home = EPD * d
+    before = EPD * (y * NZ + (z + NZ - 1) % NZ)
+    after = EPD * (y * NZ + (z + 1) % NZ)
+    up = (i // 2) % 2 == 0 if not isinstance(chunk, int) or chunk < NEAR else chunk % 2 == 0
+    ahead = (home, home + 2, after + 1, after + 3)
+    behind = (home + 1, home + 3, before, before + 2)
+    return tuple(jnp.where(up, f, g) for f, g in zip(ahead, behind))
 
 
 def kernel(
@@ -84,7 +76,7 @@
     qbuf, kbuf, vbuf, qaug, kaug, sbuf, pmax, mrow, asum, aacc, obuf,
     tok, xbuf, outbuf, arrived, res, returned, win, wout, acc, cols, spare,
     ready, loc, ksend, vsend, qsend, krecv, vrecv, qrecv, kfwd, vfwd,
-    wsem, osend, orecv, dsend, drecv, rsend, rrecv, wsend, wrecv, wsend2,
+    wsem, osend, orecv, dsend, drecv, rsend, rrecv, wsend, wrecv, wsend2, zsend, precv, bsend, fsend, rsend2, rrecv2,
 ):
     s = lax.axis_index("seq")
     e = lax.axis_index("exp")
@@ -142,13 +134,72 @@
         buf = win if part == 0 else wout
         return remote(buf.at[EPD + j], buf.at[EPD + j], wsend2.at[j], wrecv.at[part, j], other_core, e)
 
-    for part in range(2):
-
-        @pl.when(k == part)
-        def _():
-            copy_weights(part, 0).start()
-            copy_weights(part, 1).start()
-
+    def piece_of(part, x, p):
+        return (win.at[x, pl.ds(p * 64, 64)], wout.at[x, pl.ds(p * 128, 128)])[part]
+
+    def copy_piece(part, j):
+        src = (win_hbm.at[2 + j, pl.ds(c * 64, 64)], wout_hbm.at[2 + j, pl.ds(c * 128, 128)])[part]
+        z = (e % NZ + (1 if j == 0 else NZ - 1)) % NZ
+        return remote(src, piece_of(part, 6 + j, c), zsend.at[j], precv.at[part, j, c], s, e // NZ * NZ + z)
+
+    def share_piece(part, j, i):
+        piece = piece_of(part, 6 + j, c)
+        to = other_core if isinstance(i, int) else 2 * ((c + i) % SEQS) + k
+        return remote(piece, piece, bsend.at[j, i], precv.at[part, j, c], to, e)
+
+    def pass_piece(part, j, i):
+        p = (c + SEQS - i) % SEQS
+        piece = piece_of(part, 6 + j, p)
+        return remote(piece, piece, fsend.at[j, i], precv.at[part, j, p], other_core, e)
+
+    def on_part(act):
+        for part in range(2):
+            pl.when(k == part)(functools.partial(act, part))
+
+    def over_pieces(make, act):
+        def one(i, _):
+            for j in range(2):
+                act(make(j, i))
+            return 0
+
+        lax.fori_loop(1, SEQS, one, 0)
+
+    def first_weights(part):
+        for j in range(2):
+            copy_piece(part, j).start()
+        for j in range(2):
+            copy_weights(part, j).start()
+
+    def share_weights(part):
+        for j in range(2):
+            copy_piece(part, j).wait_recv()
+            share_piece(part, j, 0).start()
+        over_pieces(functools.partial(share_piece, part), lambda copy: copy.start())
+
+    def pass_pieces(part):
+        def go(copy):
+            copy.wait_recv()
+            copy.start()
+
+        over_pieces(functools.partial(pass_piece, part), go)
+
+    def take_pieces(part):
+        def one(p, _):
+            for j in range(2):
+                piece = piece_of(1 - part, 6 + j, p)
+                pltpu.make_async_copy(piece, piece, precv.at[1 - part, j, p]).wait()
+            return 0
+
+        lax.fori_loop(0, SEQS, one, 0)
+
+    def drain_pieces(part):
+        for j in range(2):
+            copy_piece(part, j).wait_send()
+            share_piece(part, j, 0).wait_send()
+        over_pieces(functools.partial(share_piece, part), lambda copy: copy.wait_send())
+        over_pieces(functools.partial(pass_piece, part), lambda copy: copy.wait_send())
+
+    on_part(first_weights)
     start_with(0)
     own = (
         pltpu.make_async_copy(k_ref.at[c], kbuf.at[s], loc.at[0]),
@@ -342,6 +393,8 @@
 
     lax.fori_loop(0, GROUPS, attend, 0)
 
+    on_part(share_weights)
+
     for part in range(2):
 
         @pl.when(k == part)
@@ -371,9 +424,7 @@
         return buf.at[pl.ds(first, count)]
 
     def sending(i):
-        return remote(
-            rows_at(outbuf, i), rows_at(arrived, i), dsend.at[i], drecv.at[i], s, partner_to(e, 14 if isinstance(i, int) and i == NE else i)
-        )
+        return remote(rows_at(outbuf, i), rows_at(arrived, i), dsend.at[i], drecv.at[i], s, partner_to(e, i))
 
     slot_line = lax.broadcasted_iota(jnp.int32, (CAP, SUB), 0)
 
@@ -383,21 +434,17 @@
         rows = jnp.dot(chosen, xbuf[...].reshape(SUB, SUB), preferred_element_type=f32)
         return rows.astype(bf16).reshape(EPD, CAP, SUB)
 
-    outbuf[0:EPD] = gathered(0)
-    sending(0).start()
-    sending(1).start()
-
     def dispatch(i, _):
-        outbuf[pl.ds(EPD * (i - 1), EPD)] = gathered(i - 1)
+        outbuf[pl.ds(EPD * i, EPD)] = gathered(i)
         sending(i).start()
         return 0
 
-    lax.fori_loop(2, NE - 1, dispatch, 0)
-    rest = gathered(NE - 1)
-    outbuf[60:62] = rest[0:2]
-    sending(NE).start()
-    arrived[62:64] = rest[2:4]
-    arrived[56:60] = gathered(NE - 2)
+    lax.fori_loop(0, NEAR, dispatch, 0)
+    outbuf[48:52] = gathered(12)
+    outbuf[52:56] = gathered(13)
+    sending(NEAR).start()
+    arrived[56:60] = gathered(14)
+    arrived[60:64] = gathered(15)
 
     logits = lax.dot_general(
         xbuf[...].reshape(SUB, SUB), rw_ref[...], (((1,), (1,)), ((), ())), preferred_element_type=f32
@@ -422,43 +469,51 @@
                 buf = (win if part == 0 else wout).at[EPD + j]
                 pltpu.make_async_copy(buf, buf, wrecv.at[part, j]).wait()
 
-    def giving(i):
+    def giving(chunk, late):
+        i = jnp.minimum(chunk, NEAR)
+        first, count = (EPD * chunk + 3, 1) if late else (EPD * chunk, 3)
         return remote(
-            rows_at(res, i), rows_at(returned, i), rsend.at[i], rrecv.at[i], s, partner_from(e, 14 if isinstance(i, int) and i == NE else i)
+            res.at[pl.ds(first, count)], returned.at[pl.ds(first, count)],
+            (rsend2 if late else rsend).at[chunk], (rrecv2 if late else rrecv).at[chunk], s, partner_from(e, i),
         )
 
-    def run_experts(blocks, first, step):
-        def one(xp, _):
-            w = first + step * xp
-            a = jnp.concatenate([arrived[at + xp] for at in blocks], axis=0)
-            u = jnp.dot(a, win[w], preferred_element_type=f32)
-            hid = 0.5 * u * (1.0 + jnp.tanh(0.7978845608028654 * (u + 0.044715 * (u * u * u))))
-            y = jnp.dot(hid.astype(bf16), wout[w], preferred_element_type=f32).astype(bf16)
-            for j in range(4):
-                res[blocks[j] + xp] = y[j * CAP:(j + 1) * CAP]
-            return 0
-
-        lax.fori_loop(0, 2, one, 0)
+    def run_expert(chunks, xp, w):
+        a = jnp.concatenate([arrived[EPD * at + xp] for at in chunks], axis=0)
+        u = jnp.dot(a, win[w], preferred_element_type=f32)
+        hid = 0.5 * u * (1.0 + jnp.tanh(0.7978845608028654 * (u + 0.044715 * (u * u * u))))
+        y = jnp.dot(hid.astype(bf16), wout[w], preferred_element_type=f32).astype(bf16)
+        for j in range(4):
+            res[EPD * chunks[j] + xp] = y[j * CAP:(j + 1) * CAP]
 
     plan = (
-        ((0, 1, 2, 3, 6, 7), (0, 2, 4, 8), (6, 10, 22, 26), (0, 1, 2, 3)),
-        ((4, 5, 8, 9), (12, 16, 20, 24), (14, 18, 30, 34), (4, 5, 6, 7)),
-        ((10, 11, 14), (28, 32, 36, 40), (38, 42, 54, 58), (8, 9, 10, 11)),
-        ((12, 13, 16), (44, 48, 52, 56), (46, 50, 60, 62), (12, 13, 14, 16)),
+        ((0, 1, 4, 5), (0, 1, 4, 5), True),
+        ((2, 3, 6, 7), (2, 3, 6, 7), False),
+        ((8, 9, 12), (8, 9, 12, 14), True),
+        ((10, 11), (10, 11, 13, 15), False),
     )
-    for q, (needed, always, shared, done) in enumerate(plan):
+    for needed, chunks, up in plan:
         for i in needed:
             part = rows_at(arrived, i)
             pltpu.make_async_copy(part, part, drecv.at[i]).wait()
-        run_experts(always, 2, 1)
-        if q % 2 == 0:
-            run_experts(shared, 0, 5)
-        else:
-            run_experts(shared, 1, 3)
-        for i in done:
-            giving(i).start()
-    returned[56:60] = res[56:60]
-    returned[62:64] = res[62:64]
+
+        def early(xp, _):
+            late = jnp.where(xp >= 2, 1, 0)
+            run_expert(chunks, xp, 2 * xp + late if up else 2 * xp + 1 - late)
+            return 0
+
+        lax.fori_loop(0, 3, early, 0)
+        for chunk in chunks:
+            if chunk < 14:
+                giving(chunk, False).start()
+
+    on_part(pass_pieces)
+    on_part(take_pieces)
+    for _, chunks, up in plan:
+        run_expert(chunks, 3, 7 if up else 6)
+        for chunk in chunks:
+            if chunk < 14:
+                giving(chunk, True).start()
+    returned[56:64] = res[56:64]
 
     lane = lax.broadcasted_iota(jnp.int32, (SUB, HD), 1)
 
@@ -479,23 +534,22 @@
     def chunk_rows(chunk):
         return returned[pl.ds(EPD * chunk, EPD)].reshape(ROWS, SUB)
 
-    def wait_rows(i):
-        part = rows_at(returned, i)
-        pltpu.make_async_copy(part, part, rrecv.at[i]).wait()
-
-    for i in (0, 1, 2):
-        wait_rows(i)
-    add_rows([table_of(0), table_of(1)], [chunk_rows(0), chunk_rows(1)])
-
-    def combine(p, _):
-        wait_rows(2 * p + 1)
-        wait_rows(2 * p + 2)
-        add_rows([table_of(2 * p), table_of(2 * p + 1)], [chunk_rows(2 * p), chunk_rows(2 * p + 1)])
-        return 0
-
-    lax.fori_loop(1, NE // 2 - 1, combine, 0)
-    wait_rows(NE)
-    add_rows([table_of(NE - 2), table_of(NE - 1)], [chunk_rows(NE - 2), chunk_rows(NE - 1)])
+    def wait_rows(chunk):
+        for first, count, sem in ((EPD * chunk, 3, rrecv), (EPD * chunk + 3, 1, rrecv2)):
+            part = returned.at[pl.ds(first, count)]
+            pltpu.make_async_copy(part, part, sem.at[chunk]).wait()
+
+    add_rows([table_of(14), table_of(15)], [chunk_rows(14), chunk_rows(15)])
+
+    def combine(a, b):
+        wait_rows(a)
+        wait_rows(b)
+        add_rows([table_of(a), table_of(b)], [chunk_rows(a), chunk_rows(b)])
+
+    for first in (0, 4, 2, 6, 8):
+        combine(first, first + 1)
+    combine(10, 11)
+    combine(12, 13)
     for b in range(SEQS):
         for g in range(4):
             mix_ref[b, :, g * SUB:(g + 1) * SUB] = acc[(b * 4 + g) * TOK:(b * 4 + g + 1) * TOK].astype(bf16)
@@ -515,12 +569,18 @@
 
     def drain_rows(i, _):
         sending(i).wait_send()
-        giving(i).wait_send()
-        return 0
-
-    for i in (0, 1, NE):
-        drain_rows(i, 0)
-    lax.fori_loop(2, NE - 1, drain_rows, 0)
+        return 0
+
+    lax.fori_loop(0, NEAR, drain_rows, 0)
+    drain_rows(NEAR, 0)
+
+    def drain_returns(chunk, _):
+        giving(chunk, False).wait_send()
+        giving(chunk, True).wait_send()
+        return 0
+
+    lax.fori_loop(0, 14, drain_returns, 0)
+    on_part(drain_pieces)
     for part in range(2):
 
         @pl.when(k == part)
@@ -562,16 +622,17 @@
             pltpu.VMEM((NE * EPD, CAP, SUB), bf16),
             pltpu.VMEM((NE * EPD, CAP, SUB), bf16),
             pltpu.VMEM((NE * EPD, CAP, SUB), bf16),
-            pltpu.VMEM((EPD + 2, SUB, FFH), bf16),
-            pltpu.VMEM((EPD + 2, FFH, SUB), bf16),
+            pltpu.VMEM((2 * EPD, SUB, FFH), bf16),
+            pltpu.VMEM((2 * EPD, FFH, SUB), bf16),
             pltpu.VMEM((SUB, SUB), f32),
             pltpu.VMEM((4, SUB, HD), f32),
             pltpu.VMEM((TOK, HD), bf16),
             pltpu.SemaphoreType.REGULAR,
             dma((3,)), dma((SEQS,)), dma((SEQS,)), dma((2 * SEQS,)),
             dma((NS,)), dma((NS,)), dma((NS,)), dma((SEQS,)), dma((SEQS,)),
-            dma((2,)), dma(()), dma((SEQS,)), dma((NE + 1,)), dma((NE + 1,)), dma((NE + 1,)), dma((NE + 1,)),
+            dma((2,)), dma(()), dma((SEQS,)), dma((NE,)), dma((NE,)), dma((NE,)), dma((NE,)),
             dma((2,)), dma((2, 2)), dma((2,)),
+            dma((2,)), dma((2, 2, SEQS)), dma((2, SEQS)), dma((2, SEQS)), dma((NE,)), dma((NE,)),
         ],
         compiler_params=pltpu.CompilerParams(
             collective_id=0, has_side_effects=True, vmem_limit_bytes=56 * 1024 * 1024

time: 144 us -> 139 us (0.965)
  Pallas kernels: 139 us -> 134 us
    pallas_call x1, Pallas kernels: 139 us -> 134 us  [body(): pl.pallas_call(kernel, out_shape=(jax.ShapeDtypeStruct((SEQS, TOK, 2048),...]
where the time goes in v5:
time: 139 us; the launch traced here: 138 us
  Pallas kernels  134 us (96%)
  local copies, waits for them, and re-layouts  3.76 us (3%)
    pallas_call x1, Pallas kernels, body(): pl.pallas_call(kernel, out_shape=(jax.ShapeDtypeStruct((SEQS, TOK, 2048),...  134 us
    unnamed x2, local copies, waits for them, and re-layouts  3.76 us

profile of v5, /device:TPU:1, one launch (start us, length us, event | category | flops | bytes accessed | tf_op | source)
XLA Modules:
  0.0 138.0 jit_solution(9314046023646166507)
XLA Ops:
  0.6 133.6 %block.1 = (bf16[8,16,2048]{2,1,0:T(8,128)(2,1)}, bf16[8,16,2048]{2,1,0:T(8,128)(2,1)}) custom-call(bf16[8,2,128,128]{3,2,1,0:T(8,128)(2,1)} %bitcast.6, bf16[8,256,128]{2,1,0:T(8,128)(2,1)} %k_ref.1, bf16[8,256,128]{2,1,0:T(8,128)(2,1)} %v_ref.1, s32[8,4096]{1,0:T(8,128)} %seg_ref.1, s32[32,2,16]{2,1,0:T(2,128)} %bitcast.8, f32[16,128]{1,0:T(8,128)} %bitcast.9, ...), custom_call_target="tpu_custom_call" | custom-call | tf_op jit(solution)/shard_map/block/pallas_call | solution.py:599
  134.2 1.9 %copy.13 = bf16[8,16,2048]{2,1,0:T(8,128)(2,1)} copy(bf16[8,16,2048]{2,1,0:T(8,128)(2,1)} %get-tuple-element.4) | data formatting | bytes 1048576
  136.1 1.9 %copy.14 = bf16[8,16,2048]{2,1,0:T(8,128)(2,1)} copy(bf16[8,16,2048]{2,1,0:T(8,128)(2,1)} %get-tuple-element.5) | data formatting | bytes 1048576

commit v6 on v5

--- a/solution.py
+++ b/solution.py
@@ -170,11 +170,15 @@
         for j in range(2):
             copy_weights(part, j).start()
 
-    def share_weights(part):
-        for j in range(2):
-            copy_piece(part, j).wait_recv()
-            share_piece(part, j, 0).start()
-        over_pieces(functools.partial(share_piece, part), lambda copy: copy.start())
+    def share_weights(j, part):
+        copy_piece(part, j).wait_recv()
+        share_piece(part, j, 0).start()
+
+        def one(i, _):
+            share_piece(part, j, i).start()
+            return 0
+
+        lax.fori_loop(1, SEQS, one, 0)
 
     def pass_pieces(part):
         def go(copy):
@@ -393,7 +397,7 @@
 
     lax.fori_loop(0, GROUPS, attend, 0)
 
-    on_part(share_weights)
+    on_part(functools.partial(share_weights, 0))
 
     for part in range(2):
 
@@ -418,6 +422,8 @@
         return 0
 
     lax.fori_loop(0, SEQS, norm, 0)
+
+    on_part(functools.partial(share_weights, 1))
 
     def rows_at(buf, i):
         first, count = region(i)
@@ -590,13 +596,18 @@
                 pass_weights(part, j).wait_send()
 
 
+def hand_on(normed_ref, mix_ref, normed_out, mix_out):
+    normed_out[...] = normed_ref[...]
+    mix_out[...] = mix_ref[...]
+
+
 def body(queries, keys, values, seg_ids, norm_gain, router_w, expert_ids, w_in, w_out):
     ids = expert_ids.transpose(1, 2, 3, 0).reshape(32, 2, TOK)
     vmem = pl.BlockSpec(memory_space=pltpu.VMEM)
     hbm = pl.BlockSpec(memory_space=pl.ANY)
     dma = pltpu.SemaphoreType.DMA
     bf16, f32 = jnp.bfloat16, jnp.float32
-    return pl.pallas_call(
+    results = pl.pallas_call(
         kernel,
         out_shape=(
             jax.ShapeDtypeStruct((SEQS, TOK, 2048), bf16),
@@ -642,6 +653,15 @@
         queries.reshape(SEQS, 2, HALF, HD), keys, values, seg_ids, ids,
         norm_gain.reshape(16, HD), router_w.T, w_in, w_out,
     )
+    tokens = pl.BlockSpec((2, TOK, 2048), lambda i: (i, 0, 0))
+    return pl.pallas_call(
+        hand_on,
+        out_shape=(jax.ShapeDtypeStruct((SEQS, TOK, 2048), bf16),) * 2,
+        grid=(SEQS // 2,),
+        in_specs=[tokens, tokens],
+        out_specs=(tokens, tokens),
+        name="hand_on",
+    )(*results)
 
 
 def solution(mesh):

time: 139 us -> 137 us (0.986)
  local copies, waits for them, and re-layouts: 3.76 us -> 0 us
  Pallas kernels: 134 us -> 136 us
    unnamed x2 -> x0, local copies, waits for them, and re-layouts: 3.76 us -> none
    pallas_call x0 -> x1, Pallas kernels: none -> 3.41 us  [body(): pl.pallas_call(hand_on, out_shape=(jax.ShapeDtypeStruct((SEQS, TOK, 2048)...]
where the time goes in v6:
time: 137 us; the launch traced here: 136 us
  Pallas kernels  136 us (99%)
    pallas_call x1, Pallas kernels, body(): pl.pallas_call(kernel, out_shape=(jax.ShapeDtypeStruct((SEQS, TOK, 2048),...  132 us
    pallas_call x1, Pallas kernels, body(): pl.pallas_call(hand_on, out_shape=(jax.ShapeDtypeStruct((SEQS, TOK, 2048)...  3.41 us

profile of v6, /device:TPU:1, one launch (start us, length us, event | category | flops | bytes accessed | tf_op | source)
XLA Modules:
  0.0 136.4 jit_solution(8509522756003897687)
XLA Ops:
  0.6 132.4 %block.1 = (bf16[8,16,2048]{2,1,0:T(8,128)(2,1)}, bf16[8,16,2048]{2,1,0:T(8,128)(2,1)}) custom-call(bf16[8,2,128,128]{3,2,1,0:T(8,128)(2,1)} %bitcast.6, bf16[8,256,128]{2,1,0:T(8,128)(2,1)} %k_ref.1, bf16[8,256,128]{2,1,0:T(8,128)(2,1)} %v_ref.1, s32[8,4096]{1,0:T(8,128)} %seg_ref.1, s32[32,2,16]{2,1,0:T(2,128)} %bitcast.8, f32[16,128]{1,0:T(8,128)} %bitcast.9, ...), custom_call_target="tpu_custom_call" | custom-call | tf_op jit(solution)/shard_map/block/pallas_call | solution.py:610
  133.0 3.4 %hand_on.1 = (bf16[8,16,2048]{2,1,0:T(8,128)(2,1)}, bf16[8,16,2048]{2,1,0:T(8,128)(2,1)}) custom-call(bf16[8,16,2048]{2,1,0:T(8,128)(2,1)} %get-tuple-element.4.normed_ref, bf16[8,16,2048]{2,1,0:T(8,128)(2,1)} %get-tuple-element.5.mix_ref), custom_call_target="tpu_custom_call" | custom-call | tf_op jit(solution)/shard_map/hand_on/pallas_call | solution.py:657
